TPU v7x, 256 devices: a whole 4x4x8 slice. The times are simulated.
256 devices in a mesh: mode: 16 (over y_hi, z), sx: 4 (over x), sy: 4 (over y_lo, core).
Axes of the slice: x: 4, y: 4 (y_hi: 2, y_lo: 2; y = y_hi * 2 + y_lo), z: 8, core: 2. Of those that a mesh axis runs over, the one named last changes fastest.
Arguments:
- start_field: float32 [2048, 16, 512], P('mode', 'sx', 'sy'), may hold values from -2.5 to 2.5
- right_side: float32 [2048, 16, 512], P('mode', 'sx', 'sy'), may hold values from -6 to 6
- mean_coef: float32 [16, 512], P('sx', 'sy'), may hold values from 0.5 to 2
- term_coef: float32 [8, 16, 512], P(None, 'sx', 'sy'), may hold values from -3 to 3
- coupling: float32 [8, 2048, 2048], P(None, None, 'mode'), may hold values from -0.05 to 0.05, as said below
- block_mask: int32 [8, 16, 16], replicated, may hold values from 0 to 1, as said below
Outputs:
- solution: float32 [2048, 16, 512], P('mode', 'sx', 'sy')
- residual: float32 [2048, 16, 512], P('mode', 'sx', 'sy')
Inputs may be any that keep to these rules, and one draw needn't show every extreme that they name: coupling[t] is symmetric: coupling[t, i, j] = coupling[t, j, i]. block_mask[t] is symmetric; entry [t, a, b] covers modes a * 128 to (a + 1) * 128 - 1 against b * 128 to (b + 1) * 128 - 1.
All inputs are finite; a program needn't handle non-finite values.
Results may differ from a plain program's by a relative error of at most 0.0002.
Values sent between devices are 32-bit elements; how exact they have to be, the bound alone decides.
A program may use at most 128 MiB of HBM per device.

v0:
```python
import jax
import jax.numpy as jnp
from jax import lax
from jax.sharding import PartitionSpec as P

SWEEPS = 3


react = 0.5
theta = 8.5
delta = 8.0


def extended(value, sides, width):
    for axis, dim in sides:
        devices, length = (lax.axis_size(axis), value.shape[dim])
        up = [(i, (i + 1) % devices) for i in range(devices)]
        down = [(j, i) for i, j in up]
        last = lax.slice_in_dim(value, length - width, length, axis=dim)
        initial = lax.slice_in_dim(value, 0, width, axis=dim)
        before = lax.ppermute(last, axis, up)
        after = lax.ppermute(initial, axis, down)
        value = jnp.concatenate([before, value, after], axis=dim)
    return value


def crop(values, margin):
    return values[..., margin:-margin, margin:-margin]


def flux_pad(coef, padded):
    width_x = padded.shape[-2] - 2
    width_y = padded.shape[-1] - 2
    center_coef = coef[..., 1:-1, 1:-1]
    center_val = padded[..., 1:-1, 1:-1]
    total = None
    for off_x, off_y in ((0, 1), (2, 1), (1, 0), (1, 2)):
        neigh_coef = coef[..., off_x : off_x + width_x, off_y : off_y + width_y]
        neigh_val = padded[..., off_x : off_x + width_x, off_y : off_y + width_y]
        term_value = 0.5 * (center_coef + neigh_coef) * (center_val - neigh_val)
        total = term_value if total is None else total + term_value
    return total


def local(start_field, right_side, mean_coef, term_coef, coupling, block_mask):
    mode_rows = start_field.shape[0]
    term_count = coupling.shape[0]
    total_modes = coupling.shape[1]
    block_count = block_mask.shape[1]
    block_size = total_modes // block_count
    sigma = theta / delta
    stacked = jnp.concatenate([mean_coef[None], term_coef], 0)
    coef_pad = extended(stacked, (("sx", 1), ("sy", 2)), SWEEPS)
    coef_one = crop(coef_pad, SWEEPS - 1)
    columns = lax.axis_index("mode") * mode_rows + jnp.arange(mode_rows, dtype=jnp.int32)
    selector = (
        jnp.arange(block_count, dtype=jnp.int32)[:, None] == (columns // block_size)[None, :]
    ).astype(jnp.float32)
    mask_cols = jnp.einsum(
        "tab,bj->taj", block_mask.astype(jnp.float32), selector, precision=lax.Precision.HIGHEST
    )
    masked = (
        coupling.reshape(term_count, block_count, block_size, mode_rows) * mask_cols[:, :, None, :]
    ).reshape(term_count, total_modes, mode_rows)
    field = start_field
    padded_field = extended(field, (("sx", 1), ("sy", 2)), 1)
    applied = flux_pad(coef_one[0], padded_field) + react * field
    mixed = jnp.einsum(
        "tji,jxy->tixy",
        masked,
        lax.all_gather(padded_field, "mode", axis=0, tiled=True),
        precision=lax.Precision.HIGHEST,
    )
    coupled = jnp.sum(flux_pad(coef_one[1:, None], mixed), axis=0)
    residual = right_side - (applied + coupled)
    rho = 1.0 / sigma
    correction = jnp.zeros(residual.shape, jnp.float32)
    direction = residual / theta
    for sweep in range(SWEEPS + 1):
        correction = correction + direction
        if sweep < SWEEPS:
            padded_corr = extended(correction, (("sx", 1), ("sy", 2)), 1)
            misfit = residual - (flux_pad(coef_one[0], padded_corr) + react * correction)
            rho_next = 1.0 / (2.0 * sigma - rho)
            direction = rho_next * rho * direction + 2.0 * rho_next / delta * misfit
            rho = rho_next
    field = field + correction
    return (field, residual)


def solution(mesh):
    placed = (
        P("mode", "sx", "sy"),
        P("mode", "sx", "sy"),
        P("sx", "sy"),
        P(None, "sx", "sy"),
        P(None, None, "mode"),
        P(),
    )
    return jax.shard_map(
        local,
        mesh=mesh,
        in_specs=placed,
        out_specs=(P("mode", "sx", "sy"), P("mode", "sx", "sy")),
        check_vma=False,
    )
```

profile of v0, /device:TPU:1, one launch (start us, length us, event | category | flops | bytes accessed | tf_op | source)
XLA Modules:
  0.0 217.8 jit_solution(1037738793580225859)
XLA Ops:
  7.2 0.0 copy-start.3
  7.2 0.0 all-gather.2.cloned.1.call-start
  7.3 1.1 copy.19
  8.4 2.1 collective-permute-start.4
  10.5 1.4 collective-permute-start.5
  11.9 1.6 collective-permute-done.4
  13.4 0.2 collective-permute-done.5
  13.6 3.3 %collective-permute-start.6 = (f32[128,6,1]{0,2,1:T(1,128)S(1)}, f32[128,6,1]{0,2,1:T(1,128)S(1)}, u32[]{:S(2)}, u32[]{:S(2)}) collective-permute-start(f32[128,6,1]{0,2,1:T(1,128)S(1)} %get-tuple-element.14), channel_id=1, source_target_pairs={{0,1},{1,2},{2,3},{3,0},{4,5},{5,6},{6,7},{7,4},{8,9},{9,10},{10,1... | collective-permute-start | bytes 9224 | tf_op jit(solution)/shard_map/ppermute | solution.py:21
  16.9 0.4 collective-permute-start.7
  17.3 0.6 collective-permute-done.6
  17.9 2.0 collective-permute-done.7
  19.9 0.8 pad_maximum_fusion
  20.8 0.0 all-gather.2.cloned.1.call-update
  20.8 0.0 copy-done.3
  20.8 0.0 copy-done.1
  20.8 1.3 collective-permute-start
  22.1 1.7 collective-permute-start.1
  23.8 1.0 collective-permute-done
  24.8 0.0 collective-permute-done.1
  24.9 0.1 fusion.97
  25.0 1.4 collective-permute-start.2
  26.4 0.1 collective-permute-start.3
  26.5 0.2 convolution_bitcast_fusion
  26.7 0.1 copy.18
  26.8 7.3 %bitcast_multiply_fusion = f32[8,2048,128]{2,1,0:T(8,128)} fusion(f32[8,2048,128]{2,1,0:T(8,128)} %param.10, f32[8,16,128]{2,1,0:T(8,128)S(1)} %convolution_bitcast_fusion), kind=kLoop, calls=%fused_computation.2 | loop fusion | flops 2097152 | bytes 16842752 | tf_op jit(solution)/shard_map/mul | solution.py:63
  34.1 0.0 collective-permute-done.2
  34.1 0.0 collective-permute-done.3
  34.1 0.1 maximum_bitcast_fusion
  34.2 0.1 fusion.72
  34.3 0.1 fusion.88
  34.4 0.1 fusion.81
  34.5 114.3 %all-gather.2.cloned.1.call-done = f32[2048,6,130]{0,2,1:T(8,128)} async-done(((f32[128,6,130]{0,2,1:T(8,128)}), f32[2048,6,130]{0,2,1:T(8,128)}) %all-gather.2.cloned.1.call-update) | async-done | bytes 6389776 | tf_op jit(solution)/shard_map/all_gather | solution.py:71
  148.8 25.0 %fusion = f32[8,128,6,130]{1,3,2,0:T(8,128)S(1)} fusion(f32[8,2048,128]{2,1,0:T(8,128)} %bitcast_multiply_fusion, f32[2048,6,130]{0,2,1:T(8,128)} %all-gather.2.cloned.1.call-done), kind=kOutput, calls=%fused_computation | convolution fusion | flops 19629342720 | bytes 17973248 | tf_op jit(solution)/shard_map/tji,jxy->tixy/dot_general | solution.py:68
  173.7 2.6 %fusion.5 = f32[128,4,128]{0,2,1:T(8,128)S(1)} fusion(f32[8,128,6,130]{1,3,2,0:T(8,128)S(1)} %fusion, f32[8,4,128]{2,1,0:T(4,128)S(1)} %get-tuple-element.29, f32[8,4,128]{2,1,0:T(4,128)S(1)} %get-tuple-element.27, f32[8,4,128]{2,1,0:T(4,128)S(1)} %get-tuple-element.28, f32[8,4,128]{2,1,0:T(4,128)S(1)} %get-tuple-element.26), kind=kLoop, calls=%fused_computation.7 | loop fusion | flops 6225920 | bytes 10813440 | tf_op jit(solution)/shard_map/reduce_sum | solution.py:74
  176.3 0.3 broadcast_multiply_fusion
  176.7 1.5 collective-permute-start.8
  178.2 1.5 collective-permute-start.9
  179.7 1.6 collective-permute-done.8
  181.3 0.0 collective-permute-done.9
  181.3 6.0 %collective-permute-start.10 = (f32[128,6,1]{0,2,1:T(1,128)S(1)}, f32[128,6,1]{0,2,1:T(1,128)S(1)}, u32[]{:S(2)}, u32[]{:S(2)}) collective-permute-start(f32[128,6,1]{0,2,1:T(1,128)S(1)} %get-tuple-element.12), channel_id=1, source_target_pairs={{0,1},{1,2},{2,3},{3,0},{4,5},{5,6},{6,7},{7,4},{8,9},{9,10},{10,1... | collective-permute-start | bytes 9224 | tf_op jit(solution)/shard_map/ppermute | solution.py:21
  187.3 0.0 collective-permute-start.11
  187.3 0.7 collective-permute-done.10
  188.0 2.3 %collective-permute-done.11 = f32[128,6,1]{0,2,1:T(1,128)S(1)} collective-permute-done((f32[128,6,1]{0,2,1:T(1,128)S(1)}, f32[128,6,1]{0,2,1:T(1,128)S(1)}, u32[]{:S(2)}, u32[]{:S(2)}) %collective-permute-start.11) | collective-permute-done | bytes 3104 | tf_op jit(solution)/shard_map/ppermute | solution.py:22
  190.3 0.3 fusion.89
  190.7 1.3 collective-permute-start.12
  192.0 1.6 collective-permute-start.13
  193.6 2.3 %collective-permute-done.12 = f32[128,1,128]{0,2,1:T(8,128)S(1)} collective-permute-done((f32[128,1,128]{0,2,1:T(8,128)S(1)}, f32[128,1,128]{0,2,1:T(8,128)S(1)}, u32[]{:S(2)}, u32[]{:S(2)}) %collective-permute-start.12) | collective-permute-done | bytes 65568 | tf_op jit(solution)/shard_map/ppermute | solution.py:21
  195.8 0.0 collective-permute-done.13
  195.8 1.2 collective-permute-start.14
  197.0 0.0 collective-permute-start.15
  197.0 0.7 collective-permute-done.14
  197.7 2.3 %collective-permute-done.15 = f32[128,6,1]{0,2,1:T(1,128)S(1)} collective-permute-done((f32[128,6,1]{0,2,1:T(1,128)S(1)}, f32[128,6,1]{0,2,1:T(1,128)S(1)}, u32[]{:S(2)}, u32[]{:S(2)}) %collective-permute-start.15) | collective-permute-done | bytes 3104 | tf_op jit(solution)/shard_map/ppermute | solution.py:22
  200.0 0.5 fusion.90
  200.5 1.0 collective-permute-start.16
  201.5 1.8 collective-permute-start.17
  203.3 2.5 %collective-permute-done.16 = f32[128,1,128]{0,2,1:T(8,128)S(1)} collective-permute-done((f32[128,1,128]{0,2,1:T(8,128)S(1)}, f32[128,1,128]{0,2,1:T(8,128)S(1)}, u32[]{:S(2)}, u32[]{:S(2)}) %collective-permute-start.16) | collective-permute-done | bytes 65568 | tf_op jit(solution)/shard_map/ppermute | solution.py:21
  205.8 0.0 collective-permute-done.17
  205.8 0.9 collective-permute-start.18
  206.7 0.0 collective-permute-start.19
  206.7 0.8 copy.21
  207.6 0.0 collective-permute-done.18
  207.6 2.2 %collective-permute-done.19 = f32[128,6,1]{0,2,1:T(1,128)S(1)} collective-permute-done((f32[128,6,1]{0,2,1:T(1,128)S(1)}, f32[128,6,1]{0,2,1:T(1,128)S(1)}, u32[]{:S(2)}, u32[]{:S(2)}) %collective-permute-start.19) | collective-permute-done | bytes 3104 | tf_op jit(solution)/shard_map/ppermute | solution.py:22
  209.7 0.3 fusion.19
  210.1 0.8 copy.20
  (16 shorter events, 0.1 us)
Async XLA Ops:
  7.2 13.6 %copy-start.3 = (f32[4,128]{1,0:T(4,128)S(1)}, f32[4,128]{1,0:T(4,128)}, u32[]{:S(2)}) copy-start(f32[4,128]{1,0:T(4,128)} %param.8) | copy-start | bytes 6148
  7.2 13.6 %copy-start.1 = (f32[8,4,128]{2,1,0:T(4,128)S(1)}, f32[8,4,128]{2,1,0:T(4,128)}, u32[]{:S(2)}) copy-start(f32[8,4,128]{2,1,0:T(4,128)} %param.9) | copy-start | bytes 49156
  7.2 19.3 %copy-start.2 = (s32[8,16,16]{2,1,0:T(8,128)S(1)}, s32[8,16,16]{2,1,0:T(8,128)}, u32[]{:S(2)}) copy-start(s32[8,16,16]{2,1,0:T(8,128)} %param.11) | copy-start | bytes 24580
  7.2 19.5 %copy-start = (f32[128,4,128]{2,1,0:T(4,128)S(1)}, f32[128,4,128]{2,1,0:T(4,128)}, u32[]{:S(2)}) copy-start(f32[128,4,128]{2,1,0:T(4,128)} %param.7) | copy-start | bytes 786436
  7.2 141.6 %all-gather.2.cloned.1.call-start = ((), (), s32[]{:S(2)}) async-start(), calls=%async_computation | async-start | bytes 7102464 | tf_op jit(solution)/shard_map/all_gather | solution.py:71
  8.4 5.0 %collective-permute-start.4 = (f32[128,1,128]{0,2,1:T(8,128)S(1)}, f32[128,1,128]{0,2,1:T(8,128)S(1)}, u32[]{:S(2)}, u32[]{:S(2)}) collective-permute-start(f32[128,1,128]{0,2,1:T(8,128)S(1)} %get-tuple-element.22), channel_id=1, source_target_pairs={{0,4},{4,8},{8,12},{12,0},{1,5},{5,9},{9,13},{13,1},{2,6},{6,10},{... | collective-permute-start | bytes 196616 | tf_op jit(solution)/shard_map/ppermute | solution.py:21
  10.5 3.1 %collective-permute-start.5 = (f32[128,1,128]{0,2,1:T(8,128)S(1)}, f32[128,1,128]{0,2,1:T(8,128)S(1)}, u32[]{:S(2)}, u32[]{:S(2)}) collective-permute-start(f32[128,1,128]{0,2,1:T(8,128)S(1)} %get-tuple-element.23), channel_id=1, source_target_pairs={{4,0},{8,4},{12,8},{0,12},{5,1},{9,5},{13,9},{1,13},{6,2},{10,6},{... | collective-permute-start | bytes 196616 | tf_op jit(solution)/shard_map/ppermute | solution.py:22
  13.6 4.3 %collective-permute-start.6 = (f32[128,6,1]{0,2,1:T(1,128)S(1)}, f32[128,6,1]{0,2,1:T(1,128)S(1)}, u32[]{:S(2)}, u32[]{:S(2)}) collective-permute-start(f32[128,6,1]{0,2,1:T(1,128)S(1)} %get-tuple-element.14), channel_id=1, source_target_pairs={{0,1},{1,2},{2,3},{3,0},{4,5},{5,6},{6,7},{7,4},{8,9},{9,10},{10,1... | collective-permute-start | bytes 9224 | tf_op jit(solution)/shard_map/ppermute | solution.py:21
  16.9 3.0 %collective-permute-start.7 = (f32[128,6,1]{0,2,1:T(1,128)S(1)}, f32[128,6,1]{0,2,1:T(1,128)S(1)}, u32[]{:S(2)}, u32[]{:S(2)}) collective-permute-start(f32[128,6,1]{0,2,1:T(1,128)S(1)} %get-tuple-element.15), channel_id=1, source_target_pairs={{1,0},{2,1},{3,2},{0,3},{5,4},{6,5},{7,6},{4,7},{9,8},{10,9},{11,1... | collective-permute-start | bytes 9224 | tf_op jit(solution)/shard_map/ppermute | solution.py:22
  20.8 4.0 %collective-permute-start = (f32[9,3,128]{2,1,0:T(4,128)S(1)}, f32[9,3,128]{2,1,0:T(4,128)S(1)}, u32[]{:S(2)}, u32[]{:S(2)}) collective-permute-start(f32[9,3,128]{2,1,0:T(4,128)S(1)} %get-tuple-element.30), channel_id=1, source_target_pairs={{0,4},{4,8},{8,12},{12,0},{1,5},{5,9},{9,13},{13,1},{2,6},{6,10},{... | collective-permute-start | bytes 41480 | tf_op jit(solution)/shard_map/ppermute | solution.py:21
  22.1 2.7 %collective-permute-start.1 = (f32[9,3,128]{2,1,0:T(4,128)S(1)}, f32[9,3,128]{2,1,0:T(4,128)S(1)}, u32[]{:S(2)}, u32[]{:S(2)}) collective-permute-start(f32[9,3,128]{2,1,0:T(4,128)S(1)} %get-tuple-element.31), channel_id=1, source_target_pairs={{4,0},{8,4},{12,8},{0,12},{5,1},{9,5},{13,9},{1,13},{6,2},{10,6},{... | collective-permute-start | bytes 41480 | tf_op jit(solution)/shard_map/ppermute | solution.py:22
  25.0 9.1 %collective-permute-start.2 = (f32[9,10,3]{2,1,0:T(8,128)S(1)}, f32[9,10,3]{2,1,0:T(8,128)S(1)}, u32[]{:S(2)}, u32[]{:S(2)}) collective-permute-start(f32[9,10,3]{2,1,0:T(8,128)S(1)} %get-tuple-element.24), channel_id=1, source_target_pairs={{0,1},{1,2},{2,3},{3,0},{4,5},{5,6},{6,7},{7,4},{8,9},{9,10},{10,1... | collective-permute-start | bytes 3248 | tf_op jit(solution)/shard_map/ppermute | solution.py:21
  26.4 7.7 %collective-permute-start.3 = (f32[9,10,3]{2,1,0:T(8,128)S(1)}, f32[9,10,3]{2,1,0:T(8,128)S(1)}, u32[]{:S(2)}, u32[]{:S(2)}) collective-permute-start(f32[9,10,3]{2,1,0:T(8,128)S(1)} %get-tuple-element.25), channel_id=1, source_target_pairs={{1,0},{2,1},{3,2},{0,3},{5,4},{6,5},{7,6},{4,7},{9,8},{10,9},{11,1... | collective-permute-start | bytes 3248 | tf_op jit(solution)/shard_map/ppermute | solution.py:22
  176.7 4.6 %collective-permute-start.8 = (f32[128,1,128]{0,2,1:T(8,128)S(1)}, f32[128,1,128]{0,2,1:T(8,128)S(1)}, u32[]{:S(2)}, u32[]{:S(2)}) collective-permute-start(f32[128,1,128]{0,2,1:T(8,128)S(1)} %get-tuple-element.20), channel_id=1, source_target_pairs={{0,4},{4,8},{8,12},{12,0},{1,5},{5,9},{9,13},{13,1},{2,6},{6,10},{... | collective-permute-start | bytes 196616 | tf_op jit(solution)/shard_map/ppermute | solution.py:21
  178.2 3.1 %collective-permute-start.9 = (f32[128,1,128]{0,2,1:T(8,128)S(1)}, f32[128,1,128]{0,2,1:T(8,128)S(1)}, u32[]{:S(2)}, u32[]{:S(2)}) collective-permute-start(f32[128,1,128]{0,2,1:T(8,128)S(1)} %get-tuple-element.21), channel_id=1, source_target_pairs={{4,0},{8,4},{12,8},{0,12},{5,1},{9,5},{13,9},{1,13},{6,2},{10,6},{... | collective-permute-start | bytes 196616 | tf_op jit(solution)/shard_map/ppermute | solution.py:22
  181.3 6.7 %collective-permute-start.10 = (f32[128,6,1]{0,2,1:T(1,128)S(1)}, f32[128,6,1]{0,2,1:T(1,128)S(1)}, u32[]{:S(2)}, u32[]{:S(2)}) collective-permute-start(f32[128,6,1]{0,2,1:T(1,128)S(1)} %get-tuple-element.12), channel_id=1, source_target_pairs={{0,1},{1,2},{2,3},{3,0},{4,5},{5,6},{6,7},{7,4},{8,9},{9,10},{10,1... | collective-permute-start | bytes 9224 | tf_op jit(solution)/shard_map/ppermute | solution.py:21
  187.3 3.0 %collective-permute-start.11 = (f32[128,6,1]{0,2,1:T(1,128)S(1)}, f32[128,6,1]{0,2,1:T(1,128)S(1)}, u32[]{:S(2)}, u32[]{:S(2)}) collective-permute-start(f32[128,6,1]{0,2,1:T(1,128)S(1)} %get-tuple-element.13), channel_id=1, source_target_pairs={{1,0},{2,1},{3,2},{0,3},{5,4},{6,5},{7,6},{4,7},{9,8},{10,9},{11,1... | collective-permute-start | bytes 9224 | tf_op jit(solution)/shard_map/ppermute | solution.py:22
  190.7 5.1 %collective-permute-start.12 = (f32[128,1,128]{0,2,1:T(8,128)S(1)}, f32[128,1,128]{0,2,1:T(8,128)S(1)}, u32[]{:S(2)}, u32[]{:S(2)}) collective-permute-start(f32[128,1,128]{0,2,1:T(8,128)S(1)} %get-tuple-element.18), channel_id=1, source_target_pairs={{0,4},{4,8},{8,12},{12,0},{1,5},{5,9},{9,13},{13,1},{2,6},{6,10},{... | collective-permute-start | bytes 196616 | tf_op jit(solution)/shard_map/ppermute | solution.py:21
  192.0 3.9 %collective-permute-start.13 = (f32[128,1,128]{0,2,1:T(8,128)S(1)}, f32[128,1,128]{0,2,1:T(8,128)S(1)}, u32[]{:S(2)}, u32[]{:S(2)}) collective-permute-start(f32[128,1,128]{0,2,1:T(8,128)S(1)} %get-tuple-element.19), channel_id=1, source_target_pairs={{4,0},{8,4},{12,8},{0,12},{5,1},{9,5},{13,9},{1,13},{6,2},{10,6},{... | collective-permute-start | bytes 196616 | tf_op jit(solution)/shard_map/ppermute | solution.py:22
  195.8 1.9 collective-permute-start.14
  197.0 3.0 %collective-permute-start.15 = (f32[128,6,1]{0,2,1:T(1,128)S(1)}, f32[128,6,1]{0,2,1:T(1,128)S(1)}, u32[]{:S(2)}, u32[]{:S(2)}) collective-permute-start(f32[128,6,1]{0,2,1:T(1,128)S(1)} %get-tuple-element.11), channel_id=1, source_target_pairs={{1,0},{2,1},{3,2},{0,3},{5,4},{6,5},{7,6},{4,7},{9,8},{10,9},{11,1... | collective-permute-start | bytes 9224 | tf_op jit(solution)/shard_map/ppermute | solution.py:22
  200.5 5.3 %collective-permute-start.16 = (f32[128,1,128]{0,2,1:T(8,128)S(1)}, f32[128,1,128]{0,2,1:T(8,128)S(1)}, u32[]{:S(2)}, u32[]{:S(2)}) collective-permute-start(f32[128,1,128]{0,2,1:T(8,128)S(1)} %get-tuple-element.16), channel_id=1, source_target_pairs={{0,4},{4,8},{8,12},{12,0},{1,5},{5,9},{9,13},{13,1},{2,6},{6,10},{... | collective-permute-start | bytes 196616 | tf_op jit(solution)/shard_map/ppermute | solution.py:21
  201.5 4.3 %collective-permute-start.17 = (f32[128,1,128]{0,2,1:T(8,128)S(1)}, f32[128,1,128]{0,2,1:T(8,128)S(1)}, u32[]{:S(2)}, u32[]{:S(2)}) collective-permute-start(f32[128,1,128]{0,2,1:T(8,128)S(1)} %get-tuple-element.17), channel_id=1, source_target_pairs={{4,0},{8,4},{12,8},{0,12},{5,1},{9,5},{13,9},{1,13},{6,2},{10,6},{... | collective-permute-start | bytes 196616 | tf_op jit(solution)/shard_map/ppermute | solution.py:22
  205.8 1.8 collective-permute-start.18
  206.7 3.0 %collective-permute-start.19 = (f32[128,6,1]{0,2,1:T(1,128)S(1)}, f32[128,6,1]{0,2,1:T(1,128)S(1)}, u32[]{:S(2)}, u32[]{:S(2)}) collective-permute-start(f32[128,6,1]{0,2,1:T(1,128)S(1)} %get-tuple-element.9), channel_id=1, source_target_pairs={{1,0},{2,1},{3,2},{0,3},{5,4},{6,5},{7,6},{4,7},{9,8},{10,9},{11,1... | collective-permute-start | bytes 9224 | tf_op jit(solution)/shard_map/ppermute | solution.py:22
Sparse Core Ops, SparseCore 0:
  20.9 127.8 all-gather.1
where the time goes:
time: 218 us
  waiting for transfers between devices  134 us (61%)
  starting transfers between devices  28.4 us (13%)
  matrix products  25.1 us (12%)
  between operations  14.2 us (7%)
  other arithmetic  12.6 us (6%)
  local copies, waits for them, and re-layouts  3.07 us (1%)
    all_gather x1, waiting for transfers between devices, local(): lax.all_gather(padded_field, 'mode', axis=0, tiled=True)  114 us
    dot_general x1, matrix products, local(): jnp.einsum('tji,jxy->tixy', masked, lax.all_gather(padded_field, 'mode',...  25 us
    ppermute x10, starting transfers between devices, extended(): before = lax.ppermute(last, axis, up)  19.8 us
    ppermute x10, waiting for transfers between devices, extended(): before = lax.ppermute(last, axis, up)  11.1 us
    ppermute x10, waiting for transfers between devices, extended(): after = lax.ppermute(initial, axis, down)  8.97 us
    ppermute x10, starting transfers between devices, extended(): after = lax.ppermute(initial, axis, down)  8.52 us
    mul x1, other arithmetic, local(): coupling.reshape(term_count, block_count, block_size, mode_rows)  7.27 us
  transfers between devices with their start and end apart: 21, of which 14 were waited for; matrix products, arithmetic and copies ran while one was open for 4% of the time, Pallas kernels for 0%

commit v1 on v0

--- a/solution.py
+++ b/solution.py
@@ -65,13 +65,10 @@
     field = start_field
     padded_field = extended(field, (("sx", 1), ("sy", 2)), 1)
     applied = flux_pad(coef_one[0], padded_field) + react * field
-    mixed = jnp.einsum(
-        "tji,jxy->tixy",
-        masked,
-        lax.all_gather(padded_field, "mode", axis=0, tiled=True),
-        precision=lax.Precision.HIGHEST,
-    )
-    coupled = jnp.sum(flux_pad(coef_one[1:, None], mixed), axis=0)
+    cells = field.shape[1] * field.shape[2]
+    fluxes = flux_pad(coef_one[1:, None], padded_field[None]).reshape(term_count, mode_rows, cells)
+    partial = jnp.einsum("tij,tjc->ic", masked, fluxes, precision=lax.Precision.HIGH)
+    coupled = lax.psum_scatter(partial, "mode", scatter_dimension=0, tiled=True).reshape(field.shape)
     residual = right_side - (applied + coupled)
     rho = 1.0 / sigma
     correction = jnp.zeros(residual.shape, jnp.float32)

time: 218 us -> 294 us (1.35)
  waiting for transfers between devices: 134 us -> 222 us
  matrix products: 25.1 us -> 11.9 us
    reduce_scatter x0 -> x1, waiting for transfers between devices: none -> 205 us  [local(): lax.psum_scatter(partial, 'mode', scatter_dimension=0, tiled=True)]
    all_gather x1 -> x0, waiting for transfers between devices: 114 us -> none  [local(): lax.all_gather(padded_field, 'mode', axis=0, tiled=True)]
    dot_general x1, matrix products: 25 us -> 10.9 us  [local(): jnp.einsum('tij,tjc->ic', masked, fluxes, precision=lax.Precision.HIGH)]
  transfers between devices with their start and end apart: 21 -> 21, of which waited for: 14 -> 13; matrix products, arithmetic and copies ran while one was open for 4% -> 4% of each run, Pallas kernels for 0% -> 0%
where the time goes in v1:
time: 294 us
  waiting for transfers between devices  222 us (76%)
  starting transfers between devices  29.3 us (10%)
  between operations  14.3 us (5%)
  matrix products  11.9 us (4%)
  other arithmetic  10.9 us (4%)
  local copies, waits for them, and re-layouts  5.53 us (2%)
    reduce_scatter x1, waiting for transfers between devices, local(): lax.psum_scatter(partial, 'mode', scatter_dimension=0, tiled=True)  205 us
    ppermute x10, starting transfers between devices, extended(): before = lax.ppermute(last, axis, up)  19.2 us
    dot_general x1, matrix products, local(): jnp.einsum('tij,tjc->ic', masked, fluxes, precision=lax.Precision.HIGH)  10.9 us
    ppermute x10, starting transfers between devices, extended(): after = lax.ppermute(initial, axis, down)  10 us
    ppermute x10, waiting for transfers between devices, extended(): after = lax.ppermute(initial, axis, down)  8.93 us
    ppermute x10, waiting for transfers between devices, extended(): before = lax.ppermute(last, axis, up)  8.27 us
    mul x1, other arithmetic, local(): coupling.reshape(term_count, block_count, block_size, mode_rows)  7.3 us
  transfers between devices with their start and end apart: 21, of which 13 were waited for; matrix products, arithmetic and copies ran while one was open for 4% of the time, Pallas kernels for 0%

profile of v1, /device:TPU:1, one launch (start us, length us, event | category | flops | bytes accessed | tf_op | source)
XLA Modules:
  0.0 294.0 jit_solution(2598559916466493294)
XLA Ops:
  7.2 0.0 reduce-scatter.2.cloned.1.call-start
  7.2 0.8 slice_maximum_fusion
  8.0 2.1 collective-permute-start
  10.1 1.4 collective-permute-start.1
  11.5 1.1 copy.24
  12.6 0.2 collective-permute-start.4
  12.8 2.6 collective-permute-start.5
  15.3 0.0 collective-permute-done
  15.4 0.0 collective-permute-done.1
  15.4 0.7 pad_maximum_fusion.32
  16.1 0.1 fusion.101
  16.2 3.2 %collective-permute-start.2 = (f32[9,10,3]{2,1,0:T(8,128)S(1)}, f32[9,10,3]{2,1,0:T(8,128)S(1)}, u32[]{:S(2)}, u32[]{:S(2)}) collective-permute-start(f32[9,10,3]{2,1,0:T(8,128)S(1)} %get-tuple-element.28), channel_id=1, source_target_pairs={{0,1},{1,2},{2,3},{3,0},{4,5},{5,6},{6,7},{7,4},{8,9},{9,10},{10,1... | collective-permute-start | bytes 3248 | tf_op jit(solution)/shard_map/ppermute | solution.py:21
  19.4 0.6 collective-permute-start.3
  20.0 1.0 convolution_bitcast_fusion.1
  21.0 0.0 copy-start.1
  21.0 0.0 copy-start.2
  21.0 7.3 %bitcast_multiply_fusion = f32[8,2048,128]{2,1,0:T(8,128)} fusion(f32[8,2048,128]{2,1,0:T(8,128)} %param.10, f32[8,16,128]{2,1,0:T(8,128)S(1)} %convolution_bitcast_fusion.1), kind=kLoop, calls=%fused_computation | loop fusion | flops 2097152 | bytes 16842752 | tf_op jit(solution)/shard_map/mul | solution.py:63
  28.3 0.1 fusion.76
  28.5 0.1 fusion.85
  28.6 0.0 collective-permute-done.4
  28.6 1.2 collective-permute-start.6
  29.8 0.6 collective-permute-start.7
  30.5 0.6 collective-permute-done.6
  31.0 2.0 collective-permute-done.7
  33.0 0.1 slice_subtract_fusion.3
  33.1 0.1 copy.18
  33.3 0.1 copy.19
  33.4 0.1 copy.20
  33.6 0.1 copy.21
  33.7 10.9 %convolution_bitcast_fusion = f32[2048,512]{1,0:T(8,128)} fusion(f32[8,2048,128]{2,1,0:T(8,128)} %bitcast_multiply_fusion, f32[128,512]{1,0:T(8,128)S(1)} %copy.21, f32[8,512]{1,0:T(8,128)S(1)} %get-tuple-element.40, f32[128,512]{1,0:T(8,128)S(1)} %copy.20, f32[8,512]{1,0:T(8,128)S(1)} %get-tuple-element.41, f32[128,512]{1,0:T(8,128)S(1)} %copy.19, ...), kind=kOutput, calls=%fused_computation.1 | convolution fusion | flops 6446120960 | bytes 13697024 | tf_op jit(solution)/shard_map/tij,tjc->ic/dot_general | solution.py:70
  44.6 0.0 reduce-scatter.2.cloned.1.call-update
  44.6 0.9 copy-done
  45.5 0.1 copy.23
  45.7 0.1 maximum_bitcast_fusion.1
  45.7 0.1 fusion.92
  45.8 204.8 %reduce-scatter.2.cloned.1.call-done = f32[128,512]{1,0:T(8,128)} async-done(((f32[2048,512]{1,0:T(8,128)}), f32[128,512]{1,0:T(8,128)}) %reduce-scatter.2.cloned.1.call-update) | async-done | bytes 262160 | tf_op jit(solution)/shard_map/reduce_scatter | solution.py:71
  250.7 1.1 copy.27
  251.8 0.3 broadcast_multiply_fusion
  252.1 1.6 collective-permute-start.8
  253.8 1.3 collective-permute-start.9
  255.1 1.6 collective-permute-done.8
  256.7 0.2 collective-permute-done.9
  256.9 6.2 %collective-permute-start.10 = (f32[128,6,1]{0,2,1:T(1,128)S(1)}, f32[128,6,1]{0,2,1:T(1,128)S(1)}, u32[]{:S(2)}, u32[]{:S(2)}) collective-permute-start(f32[128,6,1]{0,2,1:T(1,128)S(1)} %get-tuple-element.16), channel_id=1, source_target_pairs={{0,1},{1,2},{2,3},{3,0},{4,5},{5,6},{6,7},{7,4},{8,9},{9,10},{10,1... | collective-permute-start | bytes 9224 | tf_op jit(solution)/shard_map/ppermute | solution.py:21
  263.1 0.0 collective-permute-start.11
  263.1 0.7 collective-permute-done.10
  263.9 2.3 collective-permute-done.11
  266.1 0.3 fusion.93
  266.5 1.4 collective-permute-start.12
  267.9 1.5 collective-permute-start.13
  269.4 2.2 collective-permute-done.12
  271.5 0.1 collective-permute-done.13
  271.6 1.5 collective-permute-start.14
  273.1 0.0 collective-permute-start.15
  273.1 0.7 collective-permute-done.14
  273.9 2.3 collective-permute-done.15
  276.1 0.5 fusion.94
  276.6 0.7 collective-permute-start.16
  277.3 2.1 collective-permute-start.17
  279.4 2.4 collective-permute-done.16
  281.8 1.1 collective-permute-start.18
  282.9 0.8 copy.26
  283.7 2.2 collective-permute-done.19
  285.9 0.3 fusion.23
  286.3 0.8 copy.25
  (21 shorter events, 0.1 us)
Async XLA Ops:
  7.2 243.5 %reduce-scatter.2.cloned.1.call-start = ((), (), s32[]{:S(2)}) async-start(), calls=%async_computation.1 | async-start | bytes 4456448 | tf_op jit(solution)/shard_map/reduce_scatter | solution.py:71
  8.0 7.3 %collective-permute-start = (f32[9,3,128]{2,1,0:T(4,128)S(1)}, f32[9,3,128]{2,1,0:T(4,128)S(1)}, u32[]{:S(2)}, u32[]{:S(2)}) collective-permute-start(f32[9,3,128]{2,1,0:T(4,128)S(1)} %get-tuple-element.34), channel_id=1, source_target_pairs={{0,4},{4,8},{8,12},{12,0},{1,5},{5,9},{9,13},{13,1},{2,6},{6,10},{... | collective-permute-start | bytes 41480 | tf_op jit(solution)/shard_map/ppermute | solution.py:21
  10.1 5.2 %collective-permute-start.1 = (f32[9,3,128]{2,1,0:T(4,128)S(1)}, f32[9,3,128]{2,1,0:T(4,128)S(1)}, u32[]{:S(2)}, u32[]{:S(2)}) collective-permute-start(f32[9,3,128]{2,1,0:T(4,128)S(1)} %get-tuple-element.35), channel_id=1, source_target_pairs={{4,0},{8,4},{12,8},{0,12},{5,1},{9,5},{13,9},{1,13},{6,2},{10,6},{... | collective-permute-start | bytes 41480 | tf_op jit(solution)/shard_map/ppermute | solution.py:22
  12.6 16.0 %collective-permute-start.4 = (f32[128,1,128]{0,2,1:T(8,128)S(1)}, f32[128,1,128]{0,2,1:T(8,128)S(1)}, u32[]{:S(2)}, u32[]{:S(2)}) collective-permute-start(f32[128,1,128]{0,2,1:T(8,128)S(1)} %get-tuple-element.26), channel_id=1, source_target_pairs={{0,4},{4,8},{8,12},{12,0},{1,5},{5,9},{9,13},{13,1},{2,6},{6,10},{... | collective-permute-start | bytes 196616 | tf_op jit(solution)/shard_map/ppermute | solution.py:21
  12.8 15.8 %collective-permute-start.5 = (f32[128,1,128]{0,2,1:T(8,128)S(1)}, f32[128,1,128]{0,2,1:T(8,128)S(1)}, u32[]{:S(2)}, u32[]{:S(2)}) collective-permute-start(f32[128,1,128]{0,2,1:T(8,128)S(1)} %get-tuple-element.27), channel_id=1, source_target_pairs={{4,0},{8,4},{12,8},{0,12},{5,1},{9,5},{13,9},{1,13},{6,2},{10,6},{... | collective-permute-start | bytes 196616 | tf_op jit(solution)/shard_map/ppermute | solution.py:22
  16.2 12.1 %collective-permute-start.2 = (f32[9,10,3]{2,1,0:T(8,128)S(1)}, f32[9,10,3]{2,1,0:T(8,128)S(1)}, u32[]{:S(2)}, u32[]{:S(2)}) collective-permute-start(f32[9,10,3]{2,1,0:T(8,128)S(1)} %get-tuple-element.28), channel_id=1, source_target_pairs={{0,1},{1,2},{2,3},{3,0},{4,5},{5,6},{6,7},{7,4},{8,9},{9,10},{10,1... | collective-permute-start | bytes 3248 | tf_op jit(solution)/shard_map/ppermute | solution.py:21
  19.4 8.9 %collective-permute-start.3 = (f32[9,10,3]{2,1,0:T(8,128)S(1)}, f32[9,10,3]{2,1,0:T(8,128)S(1)}, u32[]{:S(2)}, u32[]{:S(2)}) collective-permute-start(f32[9,10,3]{2,1,0:T(8,128)S(1)} %get-tuple-element.29), channel_id=1, source_target_pairs={{1,0},{2,1},{3,2},{0,3},{5,4},{6,5},{7,6},{4,7},{9,8},{10,9},{11,1... | collective-permute-start | bytes 3248 | tf_op jit(solution)/shard_map/ppermute | solution.py:22
  21.0 7.3 %copy-start.1 = (f32[8,4,128]{2,1,0:T(4,128)S(1)}, f32[8,4,128]{2,1,0:T(4,128)}, u32[]{:S(2)}) copy-start(f32[8,4,128]{2,1,0:T(4,128)} %param.9) | copy-start | bytes 49156
  21.0 7.3 %copy-start.2 = (f32[4,128]{1,0:T(4,128)S(1)}, f32[4,128]{1,0:T(4,128)}, u32[]{:S(2)}) copy-start(f32[4,128]{1,0:T(4,128)} %param.8) | copy-start | bytes 6148
  28.6 2.4 collective-permute-start.6
  29.8 3.2 %collective-permute-start.7 = (f32[128,6,1]{0,2,1:T(1,128)S(1)}, f32[128,6,1]{0,2,1:T(1,128)S(1)}, u32[]{:S(2)}, u32[]{:S(2)}) collective-permute-start(f32[128,6,1]{0,2,1:T(1,128)S(1)} %get-tuple-element.19), channel_id=1, source_target_pairs={{1,0},{2,1},{3,2},{0,3},{5,4},{6,5},{7,6},{4,7},{9,8},{10,9},{11,1... | collective-permute-start | bytes 9224 | tf_op jit(solution)/shard_map/ppermute | solution.py:22
  44.6 0.9 copy-start
  252.1 4.6 %collective-permute-start.8 = (f32[128,1,128]{0,2,1:T(8,128)S(1)}, f32[128,1,128]{0,2,1:T(8,128)S(1)}, u32[]{:S(2)}, u32[]{:S(2)}) collective-permute-start(f32[128,1,128]{0,2,1:T(8,128)S(1)} %get-tuple-element.24), channel_id=1, source_target_pairs={{0,4},{4,8},{8,12},{12,0},{1,5},{5,9},{9,13},{13,1},{2,6},{6,10},{... | collective-permute-start | bytes 196616 | tf_op jit(solution)/shard_map/ppermute | solution.py:21
  253.8 3.1 %collective-permute-start.9 = (f32[128,1,128]{0,2,1:T(8,128)S(1)}, f32[128,1,128]{0,2,1:T(8,128)S(1)}, u32[]{:S(2)}, u32[]{:S(2)}) collective-permute-start(f32[128,1,128]{0,2,1:T(8,128)S(1)} %get-tuple-element.25), channel_id=1, source_target_pairs={{4,0},{8,4},{12,8},{0,12},{5,1},{9,5},{13,9},{1,13},{6,2},{10,6},{... | collective-permute-start | bytes 196616 | tf_op jit(solution)/shard_map/ppermute | solution.py:22
  256.9 7.0 %collective-permute-start.10 = (f32[128,6,1]{0,2,1:T(1,128)S(1)}, f32[128,6,1]{0,2,1:T(1,128)S(1)}, u32[]{:S(2)}, u32[]{:S(2)}) collective-permute-start(f32[128,6,1]{0,2,1:T(1,128)S(1)} %get-tuple-element.16), channel_id=1, source_target_pairs={{0,1},{1,2},{2,3},{3,0},{4,5},{5,6},{6,7},{7,4},{8,9},{9,10},{10,1... | collective-permute-start | bytes 9224 | tf_op jit(solution)/shard_map/ppermute | solution.py:21
  263.1 3.0 %collective-permute-start.11 = (f32[128,6,1]{0,2,1:T(1,128)S(1)}, f32[128,6,1]{0,2,1:T(1,128)S(1)}, u32[]{:S(2)}, u32[]{:S(2)}) collective-permute-start(f32[128,6,1]{0,2,1:T(1,128)S(1)} %get-tuple-element.17), channel_id=1, source_target_pairs={{1,0},{2,1},{3,2},{0,3},{5,4},{6,5},{7,6},{4,7},{9,8},{10,9},{11,1... | collective-permute-start | bytes 9224 | tf_op jit(solution)/shard_map/ppermute | solution.py:22
  266.5 5.0 %collective-permute-start.12 = (f32[128,1,128]{0,2,1:T(8,128)S(1)}, f32[128,1,128]{0,2,1:T(8,128)S(1)}, u32[]{:S(2)}, u32[]{:S(2)}) collective-permute-start(f32[128,1,128]{0,2,1:T(8,128)S(1)} %get-tuple-element.22), channel_id=1, source_target_pairs={{0,4},{4,8},{8,12},{12,0},{1,5},{5,9},{9,13},{13,1},{2,6},{6,10},{... | collective-permute-start | bytes 196616 | tf_op jit(solution)/shard_map/ppermute | solution.py:21
  267.9 3.7 %collective-permute-start.13 = (f32[128,1,128]{0,2,1:T(8,128)S(1)}, f32[128,1,128]{0,2,1:T(8,128)S(1)}, u32[]{:S(2)}, u32[]{:S(2)}) collective-permute-start(f32[128,1,128]{0,2,1:T(8,128)S(1)} %get-tuple-element.23), channel_id=1, source_target_pairs={{4,0},{8,4},{12,8},{0,12},{5,1},{9,5},{13,9},{1,13},{6,2},{10,6},{... | collective-permute-start | bytes 196616 | tf_op jit(solution)/shard_map/ppermute | solution.py:22
  271.6 2.3 collective-permute-start.14
  273.1 3.0 %collective-permute-start.15 = (f32[128,6,1]{0,2,1:T(1,128)S(1)}, f32[128,6,1]{0,2,1:T(1,128)S(1)}, u32[]{:S(2)}, u32[]{:S(2)}) collective-permute-start(f32[128,6,1]{0,2,1:T(1,128)S(1)} %get-tuple-element.15), channel_id=1, source_target_pairs={{1,0},{2,1},{3,2},{0,3},{5,4},{6,5},{7,6},{4,7},{9,8},{10,9},{11,1... | collective-permute-start | bytes 9224 | tf_op jit(solution)/shard_map/ppermute | solution.py:22
  276.6 5.2 %collective-permute-start.16 = (f32[128,1,128]{0,2,1:T(8,128)S(1)}, f32[128,1,128]{0,2,1:T(8,128)S(1)}, u32[]{:S(2)}, u32[]{:S(2)}) collective-permute-start(f32[128,1,128]{0,2,1:T(8,128)S(1)} %get-tuple-element.20), channel_id=1, source_target_pairs={{0,4},{4,8},{8,12},{12,0},{1,5},{5,9},{9,13},{13,1},{2,6},{6,10},{... | collective-permute-start | bytes 196616 | tf_op jit(solution)/shard_map/ppermute | solution.py:21
  277.3 4.5 %collective-permute-start.17 = (f32[128,1,128]{0,2,1:T(8,128)S(1)}, f32[128,1,128]{0,2,1:T(8,128)S(1)}, u32[]{:S(2)}, u32[]{:S(2)}) collective-permute-start(f32[128,1,128]{0,2,1:T(8,128)S(1)} %get-tuple-element.21), channel_id=1, source_target_pairs={{4,0},{8,4},{12,8},{0,12},{5,1},{9,5},{13,9},{1,13},{6,2},{10,6},{... | collective-permute-start | bytes 196616 | tf_op jit(solution)/shard_map/ppermute | solution.py:22
  281.8 1.9 collective-permute-start.18
  282.9 3.0 %collective-permute-start.19 = (f32[128,6,1]{0,2,1:T(1,128)S(1)}, f32[128,6,1]{0,2,1:T(1,128)S(1)}, u32[]{:S(2)}, u32[]{:S(2)}) collective-permute-start(f32[128,6,1]{0,2,1:T(1,128)S(1)} %get-tuple-element.13), channel_id=1, source_target_pairs={{1,0},{2,1},{3,2},{0,3},{5,4},{6,5},{7,6},{4,7},{9,8},{10,9},{11,1... | collective-permute-start | bytes 9224 | tf_op jit(solution)/shard_map/ppermute | solution.py:22
Sparse Core Ops, SparseCore 0:
  44.7 205.8 reduce-scatter.1

commit v2 on v1

v2 whole, which is shorter than its diff:
```python
import functools

import jax
import jax.numpy as jnp
from jax import lax
from jax.experimental import pallas as pl
from jax.experimental.pallas import tpu as pltpu
from jax.sharding import PartitionSpec as P

SWEEPS = 3
REACT = 0.5
THETA = 8.5
DELTA = 8.0
MESH = pl.DeviceIdType.MESH
RING = 8
GROUPS = 2
ROWS = 128
HALF = 64
WIDE = 4
LANES = 128
CELLS = WIDE * LANES
TERMS = 8

UNITS = ((0, 0, HALF, 1), (0, HALF, HALF, -1), (1, 0, HALF, 1), (1, HALF, HALF, -1))


def hops(unit, way):
    return 4 if UNITS[unit][3] == way else 3


def orders():
    lead = [(0, 4), (1, 3), (0, 3), (1, 2), (0, 2), (1, 1), (0, 1)]
    tail = [(u + 2, o) for u, o in lead]
    picks = "aabaabaaabbbbb"
    both = {"a": iter(lead), "b": iter(tail)}
    plus = [next(both[c]) for c in picks]
    minus = [(u ^ 1, o) for u, o in plus]
    return plus, minus


PLUS, MINUS = orders()
INBOX = {}
for way_, order_ in ((1, PLUS), (-1, MINUS)):
    for u_, o_ in order_:
        INBOX[(way_, u_, o_ - 1)] = len(INBOX)


def kernel(
    field, right, mean, terms, coupling, mask, sol, res,
    abuf, lhs_hi, lhs_lo, f_hi, f_lo, part, inbox, ysum, ybox,
    vp, diffs, base, coef, cbox, kd, resid, corr, edge, rowbox, colbox,
    asem, csend, crecv, hsend, hrecv, rsend, rrecv, ysend, yrecv,
):
    mode = lax.axis_index("mode")
    sx = lax.axis_index("sx")
    sy = lax.axis_index("sy")
    z = lax.rem(mode, RING)
    group = lax.div(mode, RING)
    nx, ny = 4, 4
    zp = (group * RING + lax.rem(z + 1, RING), sx, sy)
    zm = (group * RING + lax.rem(z + RING - 1, RING), sx, sy)
    partner = (lax.rem(mode + RING, 2 * RING), sx, sy)
    xp = (mode, lax.rem(sx + 1, nx), sy)
    xm = (mode, lax.rem(sx + nx - 1, nx), sy)
    yp = (mode, sx, lax.rem(sy + 1, ny))
    ym = (mode, sx, lax.rem(sy + ny - 1, ny))

    barrier = pltpu.get_barrier_semaphore()
    peers = (zp, zm, partner, xp, xm, yp, ym)
    for peer in peers:
        pl.semaphore_signal(barrier, inc=1, device_id=peer, device_id_type=MESH)

    def block_of(o, p):
        owner = group if p == 1 else 1 - group
        return owner * RING + lax.rem(z + o, RING)

    def load(o, p):
        row = pl.multiple_of(block_of(o, p) * ROWS, ROWS)
        return pltpu.make_async_copy(
            coupling.at[:, pl.ds(row, ROWS), :], abuf.at[o * 2 + p], asem.at[o * 2 + p]
        )

    for o in (4, 3, 5, 2, 6, 1, 0, 7):
        for p in (0, 1):
            load(o, p).start()

    lane = lax.broadcasted_iota(jnp.int32, (ROWS, LANES), 1)

    def edges(planes, slot):
        low, high = None, None
        for x in range(WIDE):
            lo_x = planes[x] if x == 0 else pltpu.roll(planes[x], x, 1)
            hi_x = pltpu.roll(planes[x], x + 1, 1)
            low = lo_x if x == 0 else jnp.where(lane == x, lo_x, low)
            high = hi_x if x == 0 else jnp.where(lane == x, hi_x, high)
        edge[slot, 0] = low
        edge[slot, 1] = high

    started = []

    def send(src, dst, ssem, rsem, peer):
        copy = pltpu.make_async_remote_copy(
            src_ref=src, dst_ref=dst, send_sem=ssem, recv_sem=rsem, device_id=peer, device_id_type=MESH
        )
        copy.start()
        started.append(copy)
        return copy

    def swap(slot, first, last):
        return [
            send(last, rowbox.at[slot, 0], hsend.at[slot, 0], hrecv.at[slot, 0], xp),
            send(first, rowbox.at[slot, 1], hsend.at[slot, 1], hrecv.at[slot, 1], xm),
            send(edge.at[slot, 1], colbox.at[slot, 0], hsend.at[slot, 2], hrecv.at[slot, 2], yp),
            send(edge.at[slot, 0], colbox.at[slot, 1], hsend.at[slot, 3], hrecv.at[slot, 3], ym),
        ]

    def differences(planes, slot, x):
        center = planes(x)
        up = planes(x - 1) if x > 0 else rowbox[slot, 0]
        down = planes(x + 1) if x < WIDE - 1 else rowbox[slot, 1]
        lo_col = colbox[slot, 0] if x == 0 else pltpu.roll(colbox[slot, 0], LANES - x, 1)
        hi_col = pltpu.roll(colbox[slot, 1], LANES - 1 - x, 1)
        left = jnp.where(lane == 0, lo_col, pltpu.roll(center, 1, 1))
        after = jnp.where(lane == LANES - 1, hi_col, pltpu.roll(center, LANES - 1, 1))
        return center, (center - up, center - down, center - left, center - after)

    values = []
    for x in range(WIDE):
        plane = field[pl.ds(x, ROWS, stride=WIDE), :]
        vp[x] = plane
        values.append(plane)
    edges(values, 0)
    for x in range(WIDE):
        coef[x, 0:TERMS, :] = terms[pl.ds(x, TERMS, stride=WIDE), :]
        coef[x, TERMS : 2 * TERMS, :] = jnp.broadcast_to(mean[x : x + 1, :], (TERMS, LANES))

    pl.semaphore_wait(barrier, len(peers))

    coefs = [
        send(coef, cbox.at[0], csend.at[0], crecv.at[0], xp),
        send(coef, cbox.at[1], csend.at[1], crecv.at[1], xm),
        send(coef, cbox.at[2], csend.at[2], crecv.at[2], yp),
        send(coef, cbox.at[3], csend.at[3], crecv.at[3], ym),
    ]
    halo = swap(0, vp.at[0], vp.at[WIDE - 1])

    def prepare(o):
        for p in (0, 1):
            load(o, p).wait()
            blk = block_of(o, p)
            for t in range(TERMS):
                value = abuf[o * 2 + p, t] * mask[t, blk, mode].astype(jnp.float32)
                high = value.astype(jnp.bfloat16)
                low = (value - high.astype(jnp.float32)).astype(jnp.bfloat16)
                lhs_hi[p * ROWS : (p + 1) * ROWS, t * ROWS : (t + 1) * ROWS] = high
                lhs_lo[p * ROWS : (p + 1) * ROWS, t * ROWS : (t + 1) * ROWS] = low

    def multiply(o):
        for n in range(2):
            cols = slice(n * 2 * LANES, (n + 1) * 2 * LANES)
            dot = functools.partial(jnp.dot, preferred_element_type=jnp.float32)
            total = (
                dot(lhs_hi[...], f_hi[:, cols])
                + dot(lhs_hi[...], f_lo[:, cols])
                + dot(lhs_lo[...], f_hi[:, cols])
            )
            part[o, 0, :, cols] = total[0:ROWS]
            part[o, 1, :, cols] = total[ROWS:]

    prepare(4)

    for copy in coefs:
        copy.wait_recv()
    thin = lax.broadcasted_iota(jnp.int32, (2 * TERMS, LANES), 1)
    for x in range(WIDE):
        here = coef[x]
        up = coef[x - 1] if x > 0 else cbox[0, WIDE - 1]
        down = coef[x + 1] if x < WIDE - 1 else cbox[1, 0]
        left = jnp.where(thin == 0, pltpu.roll(cbox[2, x], 1, 1), pltpu.roll(here, 1, 1))
        after = jnp.where(thin == LANES - 1, pltpu.roll(cbox[3, x], LANES - 1, 1), pltpu.roll(here, LANES - 1, 1))
        for d, other in enumerate((up, down, left, after)):
            kd[d, x] = 0.5 * (here + other)

    for copy in halo:
        copy.wait_recv()
    for x in range(WIDE):
        center, deltas = differences(lambda i: vp[i], 0, x)
        for d in range(4):
            diffs[d, x] = deltas[d]

    @pl.loop(0, TERMS)
    def _(t):
        rows = pl.ds(pl.multiple_of(t * ROWS, ROWS), ROWS)
        for x in range(WIDE):
            total = None
            for d in range(4):
                piece = kd[d, x, pl.ds(t, 1), :] * diffs[d, x]
                total = piece if total is None else total + piece
            high = total.astype(jnp.bfloat16)
            cols = slice(x * LANES, (x + 1) * LANES)
            f_hi[rows, cols] = high
            f_lo[rows, cols] = (total - high.astype(jnp.float32)).astype(jnp.bfloat16)

    multiply(4)

    ring = {}

    def forward(way, unit, o):
        p, first, count, _ = UNITS[unit]
        at = (o * way) % RING
        if o < hops(unit, way):
            ring[(way, unit, o)].wait_recv()
            part[at, p, first : first + count, :] += inbox[INBOX[(way, unit, o)]]
        i = INBOX[(way, unit, o - 1)]
        ring[(way, unit, o - 1)] = send(
            part.at[at, p, pl.ds(first, count), :],
            inbox.at[i],
            rsend.at[i],
            rrecv.at[i],
            zp if way == 1 else zm,
        )

    def collect(unit):
        p, first, count, _ = UNITS[unit]
        for way in (1, -1):
            ring[(way, unit, 0)].wait_recv()
        return (
            part[0, p, first : first + count, :]
            + inbox[INBOX[(1, unit, 0)]]
            + inbox[INBOX[(-1, unit, 0)]]
        )

    def several(count, pick):
        @pl.loop(0, count)
        def _(i):
            o = pick(i)
            prepare(o)
            multiply(o)

    swaps = []
    for slot, (one, two) in enumerate(zip(PLUS, MINUS)):
        if slot == 1:
            several(2, lambda i: 3 + 2 * i)
        if slot == 4:
            several(2, lambda i: 2 + 4 * i)
        if slot == 7:
            several(3, lambda i: lax.rem(1 + 7 * i, RING))
        forward(1, *one)
        forward(-1, *two)
        if slot == 8:
            for x in range(WIDE):
                total = REACT * vp[x]
                for d in range(4):
                    total = total + kd[d, x, TERMS : TERMS + 1, :] * diffs[d, x]
                base[x] = right[pl.ds(x, ROWS, stride=WIDE), :] - total
        if slot == 10:
            for unit in (0, 1):
                ysum[unit] = collect(unit)
                swaps.append(send(ysum.at[unit], ybox.at[unit], ysend.at[unit], yrecv.at[unit], partner))

    for unit in (2, 3):
        swaps[unit - 2].wait_recv()
        total = collect(unit) + ybox[unit - 2]
        rows = slice(UNITS[unit][1], UNITS[unit][1] + UNITS[unit][2])
        for x in range(WIDE):
            resid[x, rows, :] = base[x, rows, :] - total[:, x * LANES : (x + 1) * LANES]

    sigma = THETA / DELTA
    rho = 1.0 / sigma
    direction = []
    for x in range(WIDE):
        value = resid[x]
        res[pl.ds(x, ROWS, stride=WIDE), :] = value
        corr[0, x] = value / THETA
        diffs[0, x] = corr[0, x]
    for sweep in range(SWEEPS):
        edges([corr[sweep, x] for x in range(WIDE)], sweep + 1)
        moved = swap(sweep + 1, corr.at[sweep, 0], corr.at[sweep, WIDE - 1])
        for copy in moved:
            copy.wait_recv()
        rho_next = 1.0 / (2.0 * sigma - rho)
        for x in range(WIDE):
            center, deltas = differences(lambda i: corr[sweep, i], sweep + 1, x)
            applied = REACT * center
            for d in range(4):
                applied = applied + kd[d, x, TERMS : TERMS + 1, :] * deltas[d]
            misfit = resid[x] - applied
            step = rho_next * rho * diffs[0, x] + 2.0 * rho_next / DELTA * misfit
            if sweep < SWEEPS - 1:
                diffs[0, x] = step
                corr[sweep + 1, x] = center + step
            else:
                sol[pl.ds(x, ROWS, stride=WIDE), :] = vp[x] + (center + step)
        rho = rho_next

    for copy in started:
        copy.wait_send()


def local(start_field, right_side, mean_coef, term_coef, coupling, block_mask):
    modes, wide, lanes = start_field.shape
    f32, bf16 = jnp.float32, jnp.bfloat16
    vmem = pl.BlockSpec(memory_space=pltpu.VMEM)
    flat = jax.ShapeDtypeStruct((modes * wide, lanes), f32)
    sol, res = pl.pallas_call(
        kernel,
        out_shape=(flat, flat),
        in_specs=[
            vmem,
            vmem,
            vmem,
            vmem,
            pl.BlockSpec(memory_space=pl.ANY),
            pl.BlockSpec(memory_space=pltpu.SMEM),
        ],
        out_specs=(vmem, vmem),
        scratch_shapes=[
            pltpu.VMEM((2 * RING, TERMS, ROWS, ROWS), f32),
            pltpu.VMEM((2 * ROWS, TERMS * ROWS), bf16),
            pltpu.VMEM((2 * ROWS, TERMS * ROWS), bf16),
            pltpu.VMEM((TERMS * ROWS, CELLS), bf16),
            pltpu.VMEM((TERMS * ROWS, CELLS), bf16),
            pltpu.VMEM((RING, 2, ROWS, CELLS), f32),
            pltpu.VMEM((len(INBOX), HALF, CELLS), f32),
            pltpu.VMEM((2, HALF, CELLS), f32),
            pltpu.VMEM((2, HALF, CELLS), f32),
            pltpu.VMEM((WIDE, ROWS, LANES), f32),
            pltpu.VMEM((4, WIDE, ROWS, LANES), f32),
            pltpu.VMEM((WIDE, ROWS, LANES), f32),
            pltpu.VMEM((WIDE, 2 * TERMS, LANES), f32),
            pltpu.VMEM((4, WIDE, 2 * TERMS, LANES), f32),
            pltpu.VMEM((4, WIDE, 2 * TERMS, LANES), f32),
            pltpu.VMEM((WIDE, ROWS, LANES), f32),
            pltpu.VMEM((SWEEPS, WIDE, ROWS, LANES), f32),
            pltpu.VMEM((SWEEPS + 1, 2, ROWS, LANES), f32),
            pltpu.VMEM((SWEEPS + 1, 2, ROWS, LANES), f32),
            pltpu.VMEM((SWEEPS + 1, 2, ROWS, LANES), f32),
            pltpu.SemaphoreType.DMA((2 * RING,)),
            pltpu.SemaphoreType.DMA((4,)),
            pltpu.SemaphoreType.DMA((4,)),
            pltpu.SemaphoreType.DMA((SWEEPS + 1, 4)),
            pltpu.SemaphoreType.DMA((SWEEPS + 1, 4)),
            pltpu.SemaphoreType.DMA((len(INBOX),)),
            pltpu.SemaphoreType.DMA((len(INBOX),)),
            pltpu.SemaphoreType.DMA((2,)),
            pltpu.SemaphoreType.DMA((2,)),
        ],
        compiler_params=pltpu.CompilerParams(
            collective_id=0, has_side_effects=True, vmem_limit_bytes=48 * 1024 * 1024
        ),
        name="galerkin_step",
    )(
        start_field.reshape(modes * wide, lanes),
        right_side.reshape(modes * wide, lanes),
        mean_coef,
        term_coef.reshape(-1, lanes),
        coupling,
        block_mask,
    )
    return (sol.reshape(start_field.shape), res.reshape(start_field.shape))


def solution(mesh):
    placed = (
        P("mode", "sx", "sy"),
        P("mode", "sx", "sy"),
        P("sx", "sy"),
        P(None, "sx", "sy"),
        P(None, None, "mode"),
        P(),
    )
    return jax.shard_map(
        local,
        mesh=mesh,
        in_specs=placed,
        out_specs=(P("mode", "sx", "sy"), P("mode", "sx", "sy")),
        check_vma=False,
    )
```

time: 294 us -> 78.2 us (0.27)
  waiting for transfers between devices: 222 us -> 0 us
  Pallas kernels: 0 us -> 71.7 us
  starting transfers between devices: 29.3 us -> 0 us
  between operations: 14.3 us -> 0.65 us
  matrix products: 11.9 us -> 0 us
  other arithmetic: 10.9 us -> 0 us
    reduce_scatter x1 -> x0, waiting for transfers between devices: 205 us -> none  [local(): lax.psum_scatter(partial, 'mode', scatter_dimension=0, tiled=True)]
    pallas_call x0 -> x1, Pallas kernels: none -> 71.7 us  [local(): pl.pallas_call(kernel, out_shape=(flat, flat), in_specs=[vmem, vmem, vmem...]
    ppermute x20 -> x0, starting transfers between devices: 29.2 us -> none  [the longest x10 19.2 us: extended(): before = lax.ppermute(last, axis, up)]
    ppermute x20 -> x0, waiting for transfers between devices: 17.2 us -> none  [the longest x10 8.93 us: extended(): after = lax.ppermute(initial, axis, down)]
    dot_general x2 -> x0, matrix products: 11.9 us -> none  [the longest x1 10.9 us: local(): jnp.einsum('tij,tjc->ic', masked, fluxes, precision=lax.Precision.HIGH)]
    mul x2 -> x0, other arithmetic: 7.37 us -> none  [the longest x1 7.3 us: local(): coupling.reshape(term_count, block_count, block_size, mode_rows)]
  transfers between devices with their start and end apart: 21 -> 0, of which waited for: 13 -> 0; matrix products, arithmetic and copies ran while one was open for 4% -> 0% of each run, Pallas kernels for 0% -> 0%
where the time goes in v2:
time: 78.2 us; the launch traced here: 77.9 us
  Pallas kernels  71.7 us (92%)
  local copies, waits for them, and re-layouts  5.54 us (7%)
    pallas_call x1, Pallas kernels, local(): pl.pallas_call(kernel, out_shape=(flat, flat), in_specs=[vmem, vmem, vmem...  71.7 us
    unnamed x12, local copies, waits for them, and re-layouts  5.54 us

profile of v2, /device:TPU:1, one launch (start us, length us, event | category | flops | bytes accessed | tf_op | source)
XLA Modules:
  0.0 77.9 jit_solution(701432819182125269)
XLA Ops:
  0.6 0.0 copy-start
  0.6 0.9 %copy-done = f32[128,4,128]{2,1,0:T(4,128)S(1)} copy-done((f32[128,4,128]{2,1,0:T(4,128)S(1)}, f32[128,4,128]{2,1,0:T(4,128)}, u32[]{:S(2)}) %copy-start) | copy-done | bytes 262168
  1.6 0.0 copy-start.1
  1.6 0.9 %copy-done.1 = f32[128,4,128]{2,1,0:T(4,128)S(1)} copy-done((f32[128,4,128]{2,1,0:T(4,128)S(1)}, f32[128,4,128]{2,1,0:T(4,128)}, u32[]{:S(2)}) %copy-start.1) | copy-done | bytes 262168
  2.5 0.0 copy-start.2
  2.5 0.8 %copy-done.2 = s32[8,16,16]{2,1,0:T(8,128)S(1)} copy-done((s32[8,16,16]{2,1,0:T(8,128)S(1)}, s32[8,16,16]{2,1,0:T(8,128)}, u32[]{:S(2)}) %copy-start.2) | copy-done | bytes 8216
  3.4 0.0 copy-start.3
  3.4 0.7 copy-done.3
  4.1 0.0 copy-start.4
  4.1 0.7 copy-done.4
  4.8 71.7 %galerkin_step.1 = (f32[512,128]{1,0:T(8,128)S(1)}, f32[512,128]{1,0:T(8,128)S(1)}) custom-call(f32[512,128]{1,0:T(8,128)S(1)} %bitcast.5, f32[512,128]{1,0:T(8,128)S(1)} %bitcast.6, f32[4,128]{1,0:T(4,128)S(1)} %copy-done.4, f32[32,128]{1,0:T(8,128)S(1)} %bitcast.9, f32[8,2048,128]{2,1,0:T(8,128)} %coupling.1, s32[8,16,16]{2,1,0:T(8,128)S(1)} %copy-done.2), custom_call_target="tpu_custom_call" | custom-call | tf_op jit(solution)/shard_map/galerkin_step/pallas_call | solution.py:305
  76.5 0.7 copy.10
  77.2 0.7 copy.11
Async XLA Ops:
  0.6 1.0 %copy-start = (f32[128,4,128]{2,1,0:T(4,128)S(1)}, f32[128,4,128]{2,1,0:T(4,128)}, u32[]{:S(2)}) copy-start(f32[128,4,128]{2,1,0:T(4,128)} %param.6) | copy-start | bytes 786436
  1.6 0.9 %copy-start.1 = (f32[128,4,128]{2,1,0:T(4,128)S(1)}, f32[128,4,128]{2,1,0:T(4,128)}, u32[]{:S(2)}) copy-start(f32[128,4,128]{2,1,0:T(4,128)} %param.7) | copy-start | bytes 786436
  2.5 0.8 %copy-start.2 = (s32[8,16,16]{2,1,0:T(8,128)S(1)}, s32[8,16,16]{2,1,0:T(8,128)}, u32[]{:S(2)}) copy-start(s32[8,16,16]{2,1,0:T(8,128)} %mask.1) | copy-start | bytes 24580
  3.4 0.7 copy-start.3
  4.1 0.7 copy-start.4

commit v3 on v2

--- a/solution.py
+++ b/solution.py
@@ -21,35 +21,34 @@
 CELLS = WIDE * LANES
 TERMS = 8
 
-UNITS = ((0, 0, HALF, 1), (0, HALF, HALF, -1), (1, 0, HALF, 1), (1, HALF, HALF, -1))
+QUARTER = 32
+UNITS = tuple((p, r, QUARTER, way) for p, r in ((0, 0), (1, 0), (1, HALF)) for r, way in ((r, 1), (r + QUARTER, -1)))
+
+PLAN = (
+    ("m", 4), ("y", 4), ("z", 0, 4), ("m", 3), ("y", 3), ("z", 2, 4), ("m", 5), ("y", 5), ("z", 1, 3), ("m", 2),
+    ("y", 2), ("z", 3, 3), ("m", 6), ("y", 6), ("m", 1), ("y", 1), ("z", 0, 3), ("m", 7), ("y", 7), ("z", 2, 3),
+    ("m", 0), ("z", 4, 4), ("z", 1, 2), ("z", 3, 2), ("z", 0, 2), ("z", 5, 3), ("z", 4, 3), ("z", 1, 1), ("z", 2, 2),
+    ("z", 0, 1), ("z", 5, 2), ("z", 4, 2), ("z", 3, 1), ("b",), ("z", 2, 1), ("s",), ("y", 0), ("z", 5, 1), ("z", 4, 1),
+)
 
 
 def hops(unit, way):
     return 4 if UNITS[unit][3] == way else 3
 
 
-def orders():
-    lead = [(0, 4), (1, 3), (0, 3), (1, 2), (0, 2), (1, 1), (0, 1)]
-    tail = [(u + 2, o) for u, o in lead]
-    picks = "aabaabaaabbbbb"
-    both = {"a": iter(lead), "b": iter(tail)}
-    plus = [next(both[c]) for c in picks]
-    minus = [(u ^ 1, o) for u, o in plus]
-    return plus, minus
-
-
-PLUS, MINUS = orders()
 INBOX = {}
-for way_, order_ in ((1, PLUS), (-1, MINUS)):
-    for u_, o_ in order_:
-        INBOX[(way_, u_, o_ - 1)] = len(INBOX)
+for step_ in PLAN:
+    if step_[0] == "z":
+        INBOX[(1, step_[1], step_[2] - 1)] = len(INBOX)
+        INBOX[(-1, step_[1] ^ 1, step_[2] - 1)] = len(INBOX)
 
 
 def kernel(
-    field, right, mean, terms, coupling, mask, sol, res,
-    abuf, lhs_hi, lhs_lo, f_hi, f_lo, part, inbox, ysum, ybox,
+    field_in, right_in, mean_in, terms_in, coupling, mask_in, sol, res,
+    field, right, mean, terms, mask,
+    abuf, lhs_hi, lhs_lo, f_hi, f_lo, part, inbox, ysum, ybox, sbox,
     vp, diffs, base, coef, cbox, kd, resid, corr, edge, rowbox, colbox,
-    asem, csend, crecv, hsend, hrecv, rsend, rrecv, ysend, yrecv,
+    isem, asem, csend, crecv, hsend, hrecv, rsend, rrecv, ysend, yrecv,
 ):
     mode = lax.axis_index("mode")
     sx = lax.axis_index("sx")
@@ -70,6 +69,15 @@
     for peer in peers:
         pl.semaphore_signal(barrier, inc=1, device_id=peer, device_id_type=MESH)
 
+    fetch = [
+        pltpu.make_async_copy(src, dst, isem.at[i])
+        for i, (src, dst) in enumerate(
+            ((field_in, field), (mean_in, mean), (terms_in, terms), (mask_in, mask), (right_in, right))
+        )
+    ]
+    for copy in fetch:
+        copy.start()
+
     def block_of(o, p):
         owner = group if p == 1 else 1 - group
         return owner * RING + lax.rem(z + o, RING)
@@ -125,11 +133,14 @@
         return center, (center - up, center - down, center - left, center - after)
 
     values = []
+    fetch[0].wait()
     for x in range(WIDE):
         plane = field[pl.ds(x, ROWS, stride=WIDE), :]
         vp[x] = plane
         values.append(plane)
     edges(values, 0)
+    fetch[1].wait()
+    fetch[2].wait()
     for x in range(WIDE):
         coef[x, 0:TERMS, :] = terms[pl.ds(x, TERMS, stride=WIDE), :]
         coef[x, TERMS : 2 * TERMS, :] = jnp.broadcast_to(mean[x : x + 1, :], (TERMS, LANES))
@@ -152,21 +163,22 @@
                 value = abuf[o * 2 + p, t] * mask[t, blk, mode].astype(jnp.float32)
                 high = value.astype(jnp.bfloat16)
                 low = (value - high.astype(jnp.float32)).astype(jnp.bfloat16)
-                lhs_hi[p * ROWS : (p + 1) * ROWS, t * ROWS : (t + 1) * ROWS] = high
-                lhs_lo[p * ROWS : (p + 1) * ROWS, t * ROWS : (t + 1) * ROWS] = low
+                lhs_hi[o, p * ROWS : (p + 1) * ROWS, t * ROWS : (t + 1) * ROWS] = high
+                lhs_lo[o, p * ROWS : (p + 1) * ROWS, t * ROWS : (t + 1) * ROWS] = low
 
     def multiply(o):
         for n in range(2):
             cols = slice(n * 2 * LANES, (n + 1) * 2 * LANES)
             dot = functools.partial(jnp.dot, preferred_element_type=jnp.float32)
             total = (
-                dot(lhs_hi[...], f_hi[:, cols])
-                + dot(lhs_hi[...], f_lo[:, cols])
-                + dot(lhs_lo[...], f_hi[:, cols])
+                dot(lhs_hi[o], f_hi[:, cols])
+                + dot(lhs_hi[o], f_lo[:, cols])
+                + dot(lhs_lo[o], f_hi[:, cols])
             )
             part[o, 0, :, cols] = total[0:ROWS]
             part[o, 1, :, cols] = total[ROWS:]
 
+    fetch[3].wait()
     prepare(4)
 
     for copy in coefs:
@@ -201,13 +213,21 @@
             f_hi[rows, cols] = high
             f_lo[rows, cols] = (total - high.astype(jnp.float32)).astype(jnp.bfloat16)
 
-    multiply(4)
-
     ring = {}
+    crossing = {}
+    crossed = set()
+
+    def settle(o):
+        if o not in crossed:
+            crossed.add(o)
+            crossing[o].wait_recv()
+            part[o, 1, HALF:, :] += ybox[o]
 
     def forward(way, unit, o):
         p, first, count, _ = UNITS[unit]
         at = (o * way) % RING
+        if unit >= 4:
+            settle(at)
         if o < hops(unit, way):
             ring[(way, unit, o)].wait_recv()
             part[at, p, first : first + count, :] += inbox[INBOX[(way, unit, o)]]
@@ -230,40 +250,47 @@
             + inbox[INBOX[(-1, unit, 0)]]
         )
 
-    def several(count, pick):
-        @pl.loop(0, count)
-        def _(i):
-            o = pick(i)
-            prepare(o)
-            multiply(o)
-
-    swaps = []
-    for slot, (one, two) in enumerate(zip(PLUS, MINUS)):
-        if slot == 1:
-            several(2, lambda i: 3 + 2 * i)
-        if slot == 4:
-            several(2, lambda i: 2 + 4 * i)
-        if slot == 7:
-            several(3, lambda i: lax.rem(1 + 7 * i, RING))
-        forward(1, *one)
-        forward(-1, *two)
-        if slot == 8:
+    sums = None
+    for step in PLAN:
+        if step[0] == "m":
+            if step[1] != 4:
+                prepare(step[1])
+            multiply(step[1])
+        elif step[0] == "z":
+            forward(1, step[1], step[2])
+            forward(-1, step[1] ^ 1, step[2])
+        elif step[0] == "y":
+            o = step[1]
+            crossing[o] = send(
+                part.at[o, 0, pl.ds(HALF, HALF), :], ybox.at[o], ysend.at[o], yrecv.at[o], partner
+            )
+        elif step[0] == "s":
+            for unit in (0, 1):
+                ysum[unit * QUARTER : (unit + 1) * QUARTER] = collect(unit)
+            sums = send(ysum, sbox, ysend.at[RING], yrecv.at[RING], partner)
+        else:
+            fetch[4].wait()
             for x in range(WIDE):
                 total = REACT * vp[x]
                 for d in range(4):
                     total = total + kd[d, x, TERMS : TERMS + 1, :] * diffs[d, x]
                 base[x] = right[pl.ds(x, ROWS, stride=WIDE), :] - total
-        if slot == 10:
-            for unit in (0, 1):
-                ysum[unit] = collect(unit)
-                swaps.append(send(ysum.at[unit], ybox.at[unit], ysend.at[unit], yrecv.at[unit], partner))
-
-    for unit in (2, 3):
-        swaps[unit - 2].wait_recv()
-        total = collect(unit) + ybox[unit - 2]
-        rows = slice(UNITS[unit][1], UNITS[unit][1] + UNITS[unit][2])
+
+    def finish(unit, extra):
+        first = UNITS[unit][1]
+        rows = slice(first, first + QUARTER)
+        total = collect(unit)
+        if extra is not None:
+            total = total + extra
         for x in range(WIDE):
             resid[x, rows, :] = base[x, rows, :] - total[:, x * LANES : (x + 1) * LANES]
+
+    sums.wait_recv()
+    finish(2, sbox[0:QUARTER])
+    finish(3, sbox[QUARTER:HALF])
+    settle(0)
+    finish(4, None)
+    finish(5, None)
 
     sigma = THETA / DELTA
     rho = 1.0 / sigma
@@ -305,25 +332,24 @@
     sol, res = pl.pallas_call(
         kernel,
         out_shape=(flat, flat),
-        in_specs=[
-            vmem,
-            vmem,
-            vmem,
-            vmem,
-            pl.BlockSpec(memory_space=pl.ANY),
-            pl.BlockSpec(memory_space=pltpu.SMEM),
-        ],
+        in_specs=[pl.BlockSpec(memory_space=pltpu.HBM)] * 6,
         out_specs=(vmem, vmem),
         scratch_shapes=[
+            pltpu.VMEM((modes * wide, lanes), f32),
+            pltpu.VMEM((modes * wide, lanes), f32),
+            pltpu.VMEM(mean_coef.shape, f32),
+            pltpu.VMEM((TERMS * WIDE, lanes), f32),
+            pltpu.SMEM(block_mask.shape, jnp.int32),
             pltpu.VMEM((2 * RING, TERMS, ROWS, ROWS), f32),
-            pltpu.VMEM((2 * ROWS, TERMS * ROWS), bf16),
-            pltpu.VMEM((2 * ROWS, TERMS * ROWS), bf16),
+            pltpu.VMEM((RING, 2 * ROWS, TERMS * ROWS), bf16),
+            pltpu.VMEM((RING, 2 * ROWS, TERMS * ROWS), bf16),
             pltpu.VMEM((TERMS * ROWS, CELLS), bf16),
             pltpu.VMEM((TERMS * ROWS, CELLS), bf16),
             pltpu.VMEM((RING, 2, ROWS, CELLS), f32),
-            pltpu.VMEM((len(INBOX), HALF, CELLS), f32),
-            pltpu.VMEM((2, HALF, CELLS), f32),
-            pltpu.VMEM((2, HALF, CELLS), f32),
+            pltpu.VMEM((len(INBOX), QUARTER, CELLS), f32),
+            pltpu.VMEM((HALF, CELLS), f32),
+            pltpu.VMEM((RING, HALF, CELLS), f32),
+            pltpu.VMEM((HALF, CELLS), f32),
             pltpu.VMEM((WIDE, ROWS, LANES), f32),
             pltpu.VMEM((4, WIDE, ROWS, LANES), f32),
             pltpu.VMEM((WIDE, ROWS, LANES), f32),
@@ -335,6 +361,7 @@
             pltpu.VMEM((SWEEPS + 1, 2, ROWS, LANES), f32),
             pltpu.VMEM((SWEEPS + 1, 2, ROWS, LANES), f32),
             pltpu.VMEM((SWEEPS + 1, 2, ROWS, LANES), f32),
+            pltpu.SemaphoreType.DMA((5,)),
             pltpu.SemaphoreType.DMA((2 * RING,)),
             pltpu.SemaphoreType.DMA((4,)),
             pltpu.SemaphoreType.DMA((4,)),
@@ -342,11 +369,11 @@
             pltpu.SemaphoreType.DMA((SWEEPS + 1, 4)),
             pltpu.SemaphoreType.DMA((len(INBOX),)),
             pltpu.SemaphoreType.DMA((len(INBOX),)),
-            pltpu.SemaphoreType.DMA((2,)),
-            pltpu.SemaphoreType.DMA((2,)),
+            pltpu.SemaphoreType.DMA((RING + 1,)),
+            pltpu.SemaphoreType.DMA((RING + 1,)),
         ],
         compiler_params=pltpu.CompilerParams(
-            collective_id=0, has_side_effects=True, vmem_limit_bytes=48 * 1024 * 1024
+            collective_id=0, has_side_effects=True, vmem_limit_bytes=60 * 1024 * 1024
         ),
         name="galerkin_step",
     )(

time: 78.2 us -> 67.3 us (0.86)
  Pallas kernels: 71.7 us -> 63.1 us
  local copies, waits for them, and re-layouts: 5.54 us -> 3.34 us
    pallas_call x1, Pallas kernels: 71.7 us -> 63.1 us  [local(): pl.pallas_call(kernel, out_shape=(flat, flat), in_specs=[pl.BlockSpec(mem...]
    unnamed x12 -> x2, local copies, waits for them, and re-layouts: 5.54 us -> 3.34 us
where the time goes in v3:
time: 67.3 us; the launch traced here: 67.1 us
  Pallas kernels  63.1 us (94%)
  local copies, waits for them, and re-layouts  3.34 us (5%)
    pallas_call x1, Pallas kernels, local(): pl.pallas_call(kernel, out_shape=(flat, flat), in_specs=[pl.BlockSpec(mem...  63.1 us
    unnamed x2, local copies, waits for them, and re-layouts  3.34 us

profile of v3, /device:TPU:1, one launch (start us, length us, event | category | flops | bytes accessed | tf_op | source)
XLA Modules:
  0.0 67.1 jit_solution(1036664233041396849)
XLA Ops:
  0.6 63.1 %galerkin_step.1 = (f32[512,128]{1,0:T(8,128)}, f32[512,128]{1,0:T(8,128)}) custom-call(f32[512,128]{1,0:T(8,128)} %bitcast.5, f32[512,128]{1,0:T(8,128)} %bitcast.6, f32[4,128]{1,0:T(4,128)} %mean_in.1, f32[32,128]{1,0:T(8,128)} %bitcast.9, f32[8,2048,128]{2,1,0:T(8,128)} %coupling.1, s32[8,16,16]{2,1,0:T(8,128)} %mask_in.1), custom_call_target="tpu_custom_call" | custom-call | tf_op jit(solution)/shard_map/galerkin_step/pallas_call | solution.py:332
  63.8 1.7 %copy.10 = f32[128,4,128]{2,1,0:T(4,128)} copy(f32[128,4,128]{2,1,0:T(4,128)} %bitcast.8) | data formatting | bytes 524288
  65.4 1.7 %copy.11 = f32[128,4,128]{2,1,0:T(4,128)} copy(f32[128,4,128]{2,1,0:T(4,128)} %bitcast.7) | data formatting | bytes 524288

commit v4 on v3

--- a/solution.py
+++ b/solution.py
@@ -47,8 +47,9 @@
     field_in, right_in, mean_in, terms_in, coupling, mask_in, sol, res,
     field, right, mean, terms, mask,
     abuf, lhs_hi, lhs_lo, f_hi, f_lo, part, inbox, ysum, ybox, sbox,
-    vp, diffs, base, coef, cbox, kd, resid, corr, edge, rowbox, colbox,
-    isem, asem, csend, crecv, hsend, hrecv, rsend, rrecv, ysend, yrecv,
+    vp, diffs, base, coef, cbox, dbox, kd, kw, kpack, edge, rowbox, colbox,
+    wide, fold, foldbox, corr, direction,
+    isem, asem, csend, crecv, hsend, hrecv, rsend, rrecv, ysend, yrecv, wsend, wrecv,
 ):
     mode = lax.axis_index("mode")
     sx = lax.axis_index("sx")
@@ -63,9 +64,11 @@
     xm = (mode, lax.rem(sx + nx - 1, nx), sy)
     yp = (mode, sx, lax.rem(sy + 1, ny))
     ym = (mode, sx, lax.rem(sy + ny - 1, ny))
+    corners = ((xp[1], yp[2]), (xm[1], yp[2]), (xp[1], ym[2]), (xm[1], ym[2]))
+    corners = tuple((mode, i, j) for i, j in corners)
 
     barrier = pltpu.get_barrier_semaphore()
-    peers = (zp, zm, partner, xp, xm, yp, ym)
+    peers = (zp, zm, partner, xp, xm, yp, ym) + corners
     for peer in peers:
         pl.semaphore_signal(barrier, inc=1, device_id=peer, device_id_type=MESH)
 
@@ -94,15 +97,15 @@
 
     lane = lax.broadcasted_iota(jnp.int32, (ROWS, LANES), 1)
 
-    def edges(planes, slot):
+    def edges(planes):
         low, high = None, None
         for x in range(WIDE):
             lo_x = planes[x] if x == 0 else pltpu.roll(planes[x], x, 1)
             hi_x = pltpu.roll(planes[x], x + 1, 1)
             low = lo_x if x == 0 else jnp.where(lane == x, lo_x, low)
             high = hi_x if x == 0 else jnp.where(lane == x, hi_x, high)
-        edge[slot, 0] = low
-        edge[slot, 1] = high
+        edge[0] = low
+        edge[1] = high
 
     started = []
 
@@ -114,23 +117,15 @@
         started.append(copy)
         return copy
 
-    def swap(slot, first, last):
-        return [
-            send(last, rowbox.at[slot, 0], hsend.at[slot, 0], hrecv.at[slot, 0], xp),
-            send(first, rowbox.at[slot, 1], hsend.at[slot, 1], hrecv.at[slot, 1], xm),
-            send(edge.at[slot, 1], colbox.at[slot, 0], hsend.at[slot, 2], hrecv.at[slot, 2], yp),
-            send(edge.at[slot, 0], colbox.at[slot, 1], hsend.at[slot, 3], hrecv.at[slot, 3], ym),
-        ]
-
-    def differences(planes, slot, x):
-        center = planes(x)
-        up = planes(x - 1) if x > 0 else rowbox[slot, 0]
-        down = planes(x + 1) if x < WIDE - 1 else rowbox[slot, 1]
-        lo_col = colbox[slot, 0] if x == 0 else pltpu.roll(colbox[slot, 0], LANES - x, 1)
-        hi_col = pltpu.roll(colbox[slot, 1], LANES - 1 - x, 1)
+    def differences(x):
+        center = vp[x]
+        up = vp[x - 1] if x > 0 else rowbox[0]
+        down = vp[x + 1] if x < WIDE - 1 else rowbox[1]
+        lo_col = colbox[0] if x == 0 else pltpu.roll(colbox[0], LANES - x, 1)
+        hi_col = pltpu.roll(colbox[1], LANES - 1 - x, 1)
         left = jnp.where(lane == 0, lo_col, pltpu.roll(center, 1, 1))
         after = jnp.where(lane == LANES - 1, hi_col, pltpu.roll(center, LANES - 1, 1))
-        return center, (center - up, center - down, center - left, center - after)
+        return (center - up, center - down, center - left, center - after)
 
     values = []
     fetch[0].wait()
@@ -138,7 +133,7 @@
         plane = field[pl.ds(x, ROWS, stride=WIDE), :]
         vp[x] = plane
         values.append(plane)
-    edges(values, 0)
+    edges(values)
     fetch[1].wait()
     fetch[2].wait()
     for x in range(WIDE):
@@ -153,7 +148,17 @@
         send(coef, cbox.at[2], csend.at[2], crecv.at[2], yp),
         send(coef, cbox.at[3], csend.at[3], crecv.at[3], ym),
     ]
-    halo = swap(0, vp.at[0], vp.at[WIDE - 1])
+    halo = [
+        send(vp.at[WIDE - 1], rowbox.at[0], hsend.at[0], hrecv.at[0], xp),
+        send(vp.at[0], rowbox.at[1], hsend.at[1], hrecv.at[1], xm),
+        send(edge.at[1], colbox.at[0], hsend.at[2], hrecv.at[2], yp),
+        send(edge.at[0], colbox.at[1], hsend.at[3], hrecv.at[3], ym),
+    ]
+    mean_rows = pl.ds(TERMS, TERMS)
+    angles = [
+        send(coef.at[:, mean_rows, :], dbox.at[i], csend.at[4 + i], crecv.at[4 + i], corner)
+        for i, corner in enumerate(corners)
+    ]
 
     def prepare(o):
         for p in (0, 1):
@@ -196,9 +201,8 @@
     for copy in halo:
         copy.wait_recv()
     for x in range(WIDE):
-        center, deltas = differences(lambda i: vp[i], 0, x)
-        for d in range(4):
-            diffs[d, x] = deltas[d]
+        for d, delta in enumerate(differences(x)):
+            diffs[d, x] = delta
 
     @pl.loop(0, TERMS)
     def _(t):
@@ -249,6 +253,141 @@
             + inbox[INBOX[(1, unit, 0)]]
             + inbox[INBOX[(-1, unit, 0)]]
         )
+
+    SPAN = WIDE + 2 * SWEEPS
+    DEEP = 2 * SWEEPS
+
+    def layout(rows):
+        at = lax.broadcasted_iota(jnp.int32, (rows, LANES), 1)
+        plane = lax.shift_right_logical(at * 171, 10)
+        return at, plane, at - DEEP * plane
+
+    def gather(planes, plane):
+        total = None
+        for i, value in planes:
+            piece = pltpu.roll(value, DEEP * i + SWEEPS, 1)
+            total = piece if total is None else jnp.where(plane == i, piece, total)
+        return total
+
+    def join(before, own, after, at, column):
+        low = jnp.where(column < SWEEPS, before, own)
+        high = jnp.where(column < SWEEPS, own, after)
+        return jnp.where(at < 64, low, pltpu.roll(high, 64, 1))
+
+    def pack_shifts(pack):
+        return (
+            pltpu.roll(pack, DEEP, 1),
+            pltpu.roll(pack, LANES - DEEP, 1),
+            pltpu.roll(pack, 1, 1),
+            pltpu.roll(pack, LANES - 1, 1),
+        )
+
+    def side_columns(i, value, pack, at):
+        left = jnp.where(at == 0, pltpu.roll(pack, LANES - (DEEP * i + SWEEPS - 1), 1), pltpu.roll(value, 1, 1))
+        after = jnp.where(
+            at == LANES - 1, pltpu.roll(pack, (60 - DEEP * i) % LANES, 1), pltpu.roll(value, LANES - 1, 1)
+        )
+        return left, after
+
+    def wide_coefficients():
+        for copy in angles:
+            copy.wait_recv()
+        at, plane, column = layout(TERMS)
+        mid = slice(TERMS, 2 * TERMS)
+
+        def column_of(low, own, high):
+            rows = [(i, low(i + 1)) for i in range(SWEEPS)]
+            rows += [(SWEEPS + x, own(x)) for x in range(WIDE)]
+            return rows + [(SWEEPS + WIDE + i, high(i)) for i in range(SWEEPS)]
+
+        here = column_of(lambda x: cbox[0, x, mid], lambda x: coef[x, mid], lambda x: cbox[1, x, mid])
+        before = column_of(lambda x: dbox[0, x], lambda x: cbox[2, x, mid], lambda x: dbox[1, x])
+        after = column_of(lambda x: dbox[2, x], lambda x: cbox[3, x, mid], lambda x: dbox[3, x])
+        pack = join(gather(before, plane), gather(here, plane), gather(after, plane), at, column)
+        for d, other in enumerate(pack_shifts(pack)):
+            kpack[d] = 0.5 * (pack + other)
+        for i in range(1, SPAN - 1):
+            value = here[i][1]
+            others = (here[i - 1][1], here[i + 1][1]) + side_columns(i, value, pack, at)
+            for d, other in enumerate(others):
+                kw[d, i] = 0.5 * (value + other)
+
+    FOLD = HALF // 4
+
+    def spread(half):
+        rows = pl.ds(half * HALF, HALF)
+        at, plane, _ = layout(HALF)
+        own = gather([(x, wide[SWEEPS + x, rows, :]) for x in range(WIDE)], plane)
+        thin_at = at[0:FOLD]
+        total = None
+        for g in range(4):
+            piece = own[g * FOLD : (g + 1) * FOLD]
+            piece = pltpu.roll(piece, 32 * g, 1) if g else piece
+            total = piece if total is None else jnp.where(thin_at >= 32 * g, piece, total)
+        fold[half] = total
+        moves = [
+            (wide.at[pl.ds(WIDE, SWEEPS), rows, :], wide.at[pl.ds(0, SWEEPS), rows, :], xp),
+            (wide.at[pl.ds(SWEEPS, SWEEPS), rows, :], wide.at[pl.ds(SWEEPS + WIDE, SWEEPS), rows, :], xm),
+        ]
+        for i, peer in enumerate(corners + (yp, ym)):
+            moves.append((fold.at[half], foldbox.at[half, i], peer))
+        return [
+            send(src, dst, wsend.at[half, i], wrecv.at[half, i], peer) for i, (src, dst, peer) in enumerate(moves)
+        ]
+
+    def sweeps(half, moved):
+        for copy in moved:
+            copy.wait_recv()
+        rows = pl.ds(half * HALF, HALF)
+        at, plane, column = layout(HALF)
+
+        def unfold(i, shift):
+            return jnp.concatenate(
+                [pltpu.roll(foldbox[half, i], (shift - 32 * g) % LANES, 1) for g in range(4)], axis=0
+            )
+
+        def beside(low, mid, high):
+            total = jnp.where(plane < SWEEPS, unfold(low, -DEEP), unfold(mid, DEEP * SWEEPS))
+            return jnp.where(plane >= SWEEPS + WIDE, unfold(high, DEEP * (SWEEPS + WIDE)), total)
+
+        here = [(i, wide[i, rows, :]) for i in range(SPAN)]
+        pack = join(beside(0, 4, 1), gather(here, plane), beside(2, 5, 3), at, column)
+        wide[SPAN, rows, :] = pack
+        for i in range(SPAN + 1):
+            value = wide[i, rows, :] * (1.0 / THETA)
+            corr[0, i, rows, :] = value
+            direction[i, rows, :] = value
+
+        sigma = THETA / DELTA
+        rho = 1.0 / sigma
+        for sweep in range(SWEEPS):
+            now, later = sweep % 2, (sweep + 1) % 2
+            rho_next = 1.0 / (2.0 * sigma - rho)
+            pack = corr[now, SPAN, rows, :]
+
+            def advance(i, value, others, coefficients):
+                applied = REACT * value
+                for d in range(4):
+                    applied = applied + coefficients(d) * (value - others[d])
+                step = rho_next * rho * direction[i, rows, :]
+                step = step + (2.0 * rho_next / DELTA) * (wide[i, rows, :] - applied)
+                return step
+
+            for i in range(sweep + 1, SPAN - 1 - sweep):
+                value = corr[now, i, rows, :]
+                others = (corr[now, i - 1, rows, :], corr[now, i + 1, rows, :]) + side_columns(i, value, pack, at)
+                step = advance(i, value, others, lambda d: kw[d, i, 0:1, :])
+                if sweep < SWEEPS - 1:
+                    direction[i, rows, :] = step
+                    corr[later, i, rows, :] = value + step
+                else:
+                    x = i - SWEEPS
+                    sol[pl.ds(half * HALF * WIDE + x, HALF, stride=WIDE), :] = vp[x, rows, :] + (value + step)
+            if sweep < SWEEPS - 1:
+                step = advance(SPAN, pack, pack_shifts(pack), lambda d: kpack[d, 0:1, :])
+                direction[SPAN, rows, :] = step
+                corr[later, SPAN, rows, :] = pack + step
+            rho = rho_next
 
     sums = None
     for step in PLAN:
@@ -275,6 +414,7 @@
                 for d in range(4):
                     total = total + kd[d, x, TERMS : TERMS + 1, :] * diffs[d, x]
                 base[x] = right[pl.ds(x, ROWS, stride=WIDE), :] - total
+            wide_coefficients()
 
     def finish(unit, extra):
         first = UNITS[unit][1]
@@ -283,42 +423,20 @@
         if extra is not None:
             total = total + extra
         for x in range(WIDE):
-            resid[x, rows, :] = base[x, rows, :] - total[:, x * LANES : (x + 1) * LANES]
+            value = base[x, rows, :] - total[:, x * LANES : (x + 1) * LANES]
+            wide[SWEEPS + x, rows, :] = value
+            res[pl.ds(first * WIDE + x, QUARTER, stride=WIDE), :] = value
 
     sums.wait_recv()
     finish(2, sbox[0:QUARTER])
     finish(3, sbox[QUARTER:HALF])
+    early = spread(0)
     settle(0)
     finish(4, None)
     finish(5, None)
-
-    sigma = THETA / DELTA
-    rho = 1.0 / sigma
-    direction = []
-    for x in range(WIDE):
-        value = resid[x]
-        res[pl.ds(x, ROWS, stride=WIDE), :] = value
-        corr[0, x] = value / THETA
-        diffs[0, x] = corr[0, x]
-    for sweep in range(SWEEPS):
-        edges([corr[sweep, x] for x in range(WIDE)], sweep + 1)
-        moved = swap(sweep + 1, corr.at[sweep, 0], corr.at[sweep, WIDE - 1])
-        for copy in moved:
-            copy.wait_recv()
-        rho_next = 1.0 / (2.0 * sigma - rho)
-        for x in range(WIDE):
-            center, deltas = differences(lambda i: corr[sweep, i], sweep + 1, x)
-            applied = REACT * center
-            for d in range(4):
-                applied = applied + kd[d, x, TERMS : TERMS + 1, :] * deltas[d]
-            misfit = resid[x] - applied
-            step = rho_next * rho * diffs[0, x] + 2.0 * rho_next / DELTA * misfit
-            if sweep < SWEEPS - 1:
-                diffs[0, x] = step
-                corr[sweep + 1, x] = center + step
-            else:
-                sol[pl.ds(x, ROWS, stride=WIDE), :] = vp[x] + (center + step)
-        rho = rho_next
+    late = spread(1)
+    sweeps(0, early)
+    sweeps(1, late)
 
     for copy in started:
         copy.wait_send()
@@ -355,34 +473,47 @@
             pltpu.VMEM((WIDE, ROWS, LANES), f32),
             pltpu.VMEM((WIDE, 2 * TERMS, LANES), f32),
             pltpu.VMEM((4, WIDE, 2 * TERMS, LANES), f32),
+            pltpu.VMEM((4, WIDE, TERMS, LANES), f32),
             pltpu.VMEM((4, WIDE, 2 * TERMS, LANES), f32),
-            pltpu.VMEM((WIDE, ROWS, LANES), f32),
-            pltpu.VMEM((SWEEPS, WIDE, ROWS, LANES), f32),
-            pltpu.VMEM((SWEEPS + 1, 2, ROWS, LANES), f32),
-            pltpu.VMEM((SWEEPS + 1, 2, ROWS, LANES), f32),
-            pltpu.VMEM((SWEEPS + 1, 2, ROWS, LANES), f32),
+            pltpu.VMEM((4, WIDE + 2 * SWEEPS, TERMS, LANES), f32),
+            pltpu.VMEM((4, TERMS, LANES), f32),
+            pltpu.VMEM((2, ROWS, LANES), f32),
+            pltpu.VMEM((2, ROWS, LANES), f32),
+            pltpu.VMEM((2, ROWS, LANES), f32),
+            pltpu.VMEM((WIDE + 2 * SWEEPS + 1, ROWS, LANES), f32),
+            pltpu.VMEM((2, HALF // 4, LANES), f32),
+            pltpu.VMEM((2, 6, HALF // 4, LANES), f32),
+            pltpu.VMEM((2, WIDE + 2 * SWEEPS + 1, ROWS, LANES), f32),
+            pltpu.VMEM((WIDE + 2 * SWEEPS + 1, ROWS, LANES), f32),
             pltpu.SemaphoreType.DMA((5,)),
             pltpu.SemaphoreType.DMA((2 * RING,)),
+            pltpu.SemaphoreType.DMA((8,)),
+            pltpu.SemaphoreType.DMA((8,)),
             pltpu.SemaphoreType.DMA((4,)),
             pltpu.SemaphoreType.DMA((4,)),
-            pltpu.SemaphoreType.DMA((SWEEPS + 1, 4)),
-            pltpu.SemaphoreType.DMA((SWEEPS + 1, 4)),
             pltpu.SemaphoreType.DMA((len(INBOX),)),
             pltpu.SemaphoreType.DMA((len(INBOX),)),
             pltpu.SemaphoreType.DMA((RING + 1,)),
             pltpu.SemaphoreType.DMA((RING + 1,)),
+            pltpu.SemaphoreType.DMA((2, 8)),
+            pltpu.SemaphoreType.DMA((2, 8)),
         ],
         compiler_params=pltpu.CompilerParams(
-            collective_id=0, has_side_effects=True, vmem_limit_bytes=60 * 1024 * 1024
+            collective_id=0, has_side_effects=True, vmem_limit_bytes=48000 * 1024
         ),
         name="galerkin_step",
     )(
-        start_field.reshape(modes * wide, lanes),
-        right_side.reshape(modes * wide, lanes),
-        mean_coef,
-        term_coef.reshape(-1, lanes),
-        coupling,
-        block_mask,
+        *(
+            pltpu.with_memory_space_constraint(value, pltpu.HBM)
+            for value in (
+                start_field.reshape(modes * wide, lanes),
+                right_side.reshape(modes * wide, lanes),
+                mean_coef,
+                term_coef.reshape(-1, lanes),
+                coupling,
+                block_mask,
+            )
+        )
     )
     return (sol.reshape(start_field.shape), res.reshape(start_field.shape))
 

time: 67.3 us -> 59.8 us (0.89)
  Pallas kernels: 63.1 us -> 57.6 us
  local copies, waits for them, and re-layouts: 3.34 us -> 1.41 us
    pallas_call x1, Pallas kernels: 63.1 us -> 57.6 us  [local(): pl.pallas_call(kernel, out_shape=(flat, flat), in_specs=[pl.BlockSpec(mem...]
    unnamed x2, local copies, waits for them, and re-layouts: 3.34 us -> 1.41 us
where the time goes in v4:
time: 59.8 us; the launch traced here: 59.7 us
  Pallas kernels  57.6 us (96%)
  local copies, waits for them, and re-layouts  1.41 us (2%)
  between operations  0.64 us (1%)
    pallas_call x1, Pallas kernels, local(): pl.pallas_call(kernel, out_shape=(flat, flat), in_specs=[pl.BlockSpec(mem...  57.6 us
    unnamed x2, local copies, waits for them, and re-layouts  1.41 us

profile of v4, /device:TPU:1, one launch (start us, length us, event | category | flops | bytes accessed | tf_op | source)
XLA Modules:
  0.0 59.7 jit_solution(3757186629080911551)
XLA Ops:
  0.6 57.6 %galerkin_step.1 = (f32[512,128]{1,0:T(8,128)S(1)}, f32[512,128]{1,0:T(8,128)S(1)}) custom-call(f32[512,128]{1,0:T(8,128)} %bitcast.7, f32[512,128]{1,0:T(8,128)} %bitcast.8, f32[4,128]{1,0:T(4,128)} %mean_in.1, f32[32,128]{1,0:T(8,128)} %bitcast.9, f32[8,2048,128]{2,1,0:T(8,128)} %coupling.1, s32[8,16,16]{2,1,0:T(8,128)} %mask_in.1), custom_call_target="tpu_custom_call" | custom-call | tf_op jit(solution)/shard_map/galerkin_step/pallas_call | solution.py:450
  58.3 0.7 %copy.10 = f32[128,4,128]{2,1,0:T(4,128)} copy(f32[128,4,128]{2,1,0:T(4,128)S(1)} %bitcast.6) | data formatting | bytes 524288
  59.0 0.7 %copy.11 = f32[128,4,128]{2,1,0:T(4,128)} copy(f32[128,4,128]{2,1,0:T(4,128)S(1)} %bitcast.5) | data formatting | bytes 524288

commit v5 on v4

--- a/solution.py
+++ b/solution.py
@@ -25,10 +25,16 @@
 UNITS = tuple((p, r, QUARTER, way) for p, r in ((0, 0), (1, 0), (1, HALF)) for r, way in ((r, 1), (r + QUARTER, -1)))
 
 PLAN = (
-    ("m", 4), ("y", 4), ("z", 0, 4), ("m", 3), ("y", 3), ("z", 2, 4), ("m", 5), ("y", 5), ("z", 1, 3), ("m", 2),
-    ("y", 2), ("z", 3, 3), ("m", 6), ("y", 6), ("m", 1), ("y", 1), ("z", 0, 3), ("m", 7), ("y", 7), ("z", 2, 3),
-    ("m", 0), ("z", 4, 4), ("z", 1, 2), ("z", 3, 2), ("z", 0, 2), ("z", 5, 3), ("z", 4, 3), ("z", 1, 1), ("z", 2, 2),
-    ("z", 0, 1), ("z", 5, 2), ("z", 4, 2), ("z", 3, 1), ("b",), ("z", 2, 1), ("s",), ("y", 0), ("z", 5, 1), ("z", 4, 1),
+    ("m", 4, 0), ("y", 4), ("z", 1, 0, 4), ("z", -1, 1, 4), ("m", 4, 1), ("z", 1, 2, 4), ("z", -1, 3, 4),
+    ("m", 3, 2), ("y", 3), ("z", 1, 3, 3), ("m", 5, 2), ("y", 5), ("z", -1, 0, 3), ("z", 1, 1, 3), ("z", -1, 2, 3),
+    ("m", 2, 2), ("y", 2), ("m", 6, 2), ("y", 6), ("z", 1, 0, 3), ("z", -1, 1, 3), ("m", 1, 2), ("y", 1),
+    ("z", 1, 4, 4), ("z", -1, 5, 4), ("m", 7, 2), ("y", 7), ("z", 1, 2, 3), ("z", -1, 3, 3), ("m", 0, 2),
+    ("z", -1, 0, 2), ("z", 1, 3, 2), ("b",), ("z", 1, 1, 2), ("z", -1, 2, 2), ("z", 1, 0, 2), ("z", -1, 1, 2),
+    ("z", 1, 4, 3), ("z", -1, 4, 3), ("z", 1, 5, 3), ("z", -1, 5, 3), ("z", 1, 2, 2), ("z", -1, 0, 1),
+    ("z", 1, 1, 1), ("z", -1, 3, 2), ("z", 1, 0, 1), ("z", -1, 1, 1), ("y", 0), ("z", 1, 4, 2), ("z", -1, 4, 2),
+    ("z", 1, 5, 2), ("z", -1, 5, 2), ("z", 1, 2, 1), ("z", -1, 2, 1), ("z", 1, 3, 1), ("z", -1, 3, 1), ("s", 0),
+    ("s", 1), ("z", 1, 4, 1), ("z", -1, 4, 1), ("z", 1, 5, 1), ("z", -1, 5, 1), ("f", 0), ("f", 1), ("f", 2),
+    ("f", 3), ("c", 0), ("c", 1), ("c", 2), ("c", 3),
 )
 
 
@@ -39,17 +45,16 @@
 INBOX = {}
 for step_ in PLAN:
     if step_[0] == "z":
-        INBOX[(1, step_[1], step_[2] - 1)] = len(INBOX)
-        INBOX[(-1, step_[1] ^ 1, step_[2] - 1)] = len(INBOX)
+        INBOX[(step_[1], step_[2], step_[3] - 1)] = len(INBOX)
 
 
 def kernel(
     field_in, right_in, mean_in, terms_in, coupling, mask_in, sol, res,
     field, right, mean, terms, mask,
     abuf, lhs_hi, lhs_lo, f_hi, f_lo, part, inbox, ysum, ybox, sbox,
-    vp, diffs, base, coef, cbox, dbox, kd, kw, kpack, edge, rowbox, colbox,
+    vp, diffs, base, coef, mrow, cxbox, cybox, mbox, kd, kw, kpack, edge, rowbox, colbox,
     wide, fold, foldbox, corr, direction,
-    isem, asem, csend, crecv, hsend, hrecv, rsend, rrecv, ysend, yrecv, wsend, wrecv,
+    isem, asem, csend, crecv, msend, mrecv, hsend, hrecv, rsend, rrecv, ysend, yrecv, wsend, wrecv,
 ):
     mode = lax.axis_index("mode")
     sx = lax.axis_index("sx")
@@ -137,16 +142,20 @@
     fetch[1].wait()
     fetch[2].wait()
     for x in range(WIDE):
-        coef[x, 0:TERMS, :] = terms[pl.ds(x, TERMS, stride=WIDE), :]
-        coef[x, TERMS : 2 * TERMS, :] = jnp.broadcast_to(mean[x : x + 1, :], (TERMS, LANES))
+        coef[x] = terms[pl.ds(x, TERMS, stride=WIDE), :]
+    mrow[0:WIDE] = mean[...]
+    mrow[WIDE:] = mean[...]
 
     pl.semaphore_wait(barrier, len(peers))
 
     coefs = [
-        send(coef, cbox.at[0], csend.at[0], crecv.at[0], xp),
-        send(coef, cbox.at[1], csend.at[1], crecv.at[1], xm),
-        send(coef, cbox.at[2], csend.at[2], crecv.at[2], yp),
-        send(coef, cbox.at[3], csend.at[3], crecv.at[3], ym),
+        send(coef.at[WIDE - 1], cxbox.at[0], csend.at[0], crecv.at[0], xp),
+        send(coef.at[0], cxbox.at[1], csend.at[1], crecv.at[1], xm),
+        send(coef, cybox.at[0], csend.at[2], crecv.at[2], yp),
+        send(coef, cybox.at[1], csend.at[3], crecv.at[3], ym),
+    ]
+    means = [
+        send(mrow, mbox.at[i], msend.at[i], mrecv.at[i], peer) for i, peer in enumerate((xp, xm, yp, ym))
     ]
     halo = [
         send(vp.at[WIDE - 1], rowbox.at[0], hsend.at[0], hrecv.at[0], xp),
@@ -154,10 +163,8 @@
         send(edge.at[1], colbox.at[0], hsend.at[2], hrecv.at[2], yp),
         send(edge.at[0], colbox.at[1], hsend.at[3], hrecv.at[3], ym),
     ]
-    mean_rows = pl.ds(TERMS, TERMS)
     angles = [
-        send(coef.at[:, mean_rows, :], dbox.at[i], csend.at[4 + i], crecv.at[4 + i], corner)
-        for i, corner in enumerate(corners)
+        send(mrow, mbox.at[4 + i], msend.at[4 + i], mrecv.at[4 + i], corner) for i, corner in enumerate(corners)
     ]
 
     def prepare(o):
@@ -171,51 +178,72 @@
                 lhs_hi[o, p * ROWS : (p + 1) * ROWS, t * ROWS : (t + 1) * ROWS] = high
                 lhs_lo[o, p * ROWS : (p + 1) * ROWS, t * ROWS : (t + 1) * ROWS] = low
 
-    def multiply(o):
+    def multiply(o, parts):
+        first, last = parts[0] * ROWS, (parts[-1] + 1) * ROWS
         for n in range(2):
             cols = slice(n * 2 * LANES, (n + 1) * 2 * LANES)
             dot = functools.partial(jnp.dot, preferred_element_type=jnp.float32)
             total = (
-                dot(lhs_hi[o], f_hi[:, cols])
-                + dot(lhs_hi[o], f_lo[:, cols])
-                + dot(lhs_lo[o], f_hi[:, cols])
+                dot(lhs_hi[o, first:last], f_hi[:, cols])
+                + dot(lhs_hi[o, first:last], f_lo[:, cols])
+                + dot(lhs_lo[o, first:last], f_hi[:, cols])
             )
-            part[o, 0, :, cols] = total[0:ROWS]
-            part[o, 1, :, cols] = total[ROWS:]
+            for i, p in enumerate(parts):
+                part[o, p, :, cols] = total[i * ROWS : (i + 1) * ROWS]
 
     fetch[3].wait()
     prepare(4)
 
-    for copy in coefs:
+    for copy in coefs + means:
         copy.wait_recv()
-    thin = lax.broadcasted_iota(jnp.int32, (2 * TERMS, LANES), 1)
+
+    def mean_plane(box, x):
+        return jnp.broadcast_to(box[x : x + 1, :], (TERMS, LANES))
+
+    thin = lax.broadcasted_iota(jnp.int32, (TERMS, LANES), 1)
+
+    def coefficients(x, rows, own, low, high, before, after):
+        up = own(x - 1) if x > 0 else low
+        down = own(x + 1) if x < WIDE - 1 else high
+        here = own(x)
+        left = jnp.where(thin == 0, pltpu.roll(before(x), 1, 1), pltpu.roll(here, 1, 1))
+        right_of = jnp.where(thin == LANES - 1, pltpu.roll(after(x), LANES - 1, 1), pltpu.roll(here, LANES - 1, 1))
+        for d, other in enumerate((up, down, left, right_of)):
+            kd[d, x, rows, :] = 0.5 * (here + other)
+
     for x in range(WIDE):
-        here = coef[x]
-        up = coef[x - 1] if x > 0 else cbox[0, WIDE - 1]
-        down = coef[x + 1] if x < WIDE - 1 else cbox[1, 0]
-        left = jnp.where(thin == 0, pltpu.roll(cbox[2, x], 1, 1), pltpu.roll(here, 1, 1))
-        after = jnp.where(thin == LANES - 1, pltpu.roll(cbox[3, x], LANES - 1, 1), pltpu.roll(here, LANES - 1, 1))
-        for d, other in enumerate((up, down, left, after)):
-            kd[d, x] = 0.5 * (here + other)
-
-    for copy in halo:
-        copy.wait_recv()
-    for x in range(WIDE):
-        for d, delta in enumerate(differences(x)):
-            diffs[d, x] = delta
-
-    @pl.loop(0, TERMS)
-    def _(t):
-        rows = pl.ds(pl.multiple_of(t * ROWS, ROWS), ROWS)
-        for x in range(WIDE):
-            total = None
-            for d in range(4):
-                piece = kd[d, x, pl.ds(t, 1), :] * diffs[d, x]
-                total = piece if total is None else total + piece
-            high = total.astype(jnp.bfloat16)
-            cols = slice(x * LANES, (x + 1) * LANES)
-            f_hi[rows, cols] = high
-            f_lo[rows, cols] = (total - high.astype(jnp.float32)).astype(jnp.bfloat16)
+        coefficients(
+            x, slice(0, TERMS), lambda i: coef[i], cxbox[0], cxbox[1], lambda i: cybox[0, i], lambda i: cybox[1, i]
+        )
+        coefficients(
+            x,
+            slice(TERMS, 2 * TERMS),
+            lambda i: mean_plane(mrow, i),
+            mean_plane(mbox.at[0], WIDE - 1),
+            mean_plane(mbox.at[1], 0),
+            lambda i: mean_plane(mbox.at[2], i),
+            lambda i: mean_plane(mbox.at[3], i),
+        )
+
+    for copies, planes in ((halo[2:], (1, 2)), (halo[:2], (0, 3))):
+        for copy in copies:
+            copy.wait_recv()
+        for x in planes:
+            for d, delta in enumerate(differences(x)):
+                diffs[d, x] = delta
+
+        @pl.loop(0, TERMS)
+        def _(t, planes=planes):
+            rows = pl.ds(pl.multiple_of(t * ROWS, ROWS), ROWS)
+            for x in planes:
+                total = None
+                for d in range(4):
+                    piece = kd[d, x, pl.ds(t, 1), :] * diffs[d, x]
+                    total = piece if total is None else total + piece
+                high = total.astype(jnp.bfloat16)
+                cols = slice(x * LANES, (x + 1) * LANES)
+                f_hi[rows, cols] = high
+                f_lo[rows, cols] = (total - high.astype(jnp.float32)).astype(jnp.bfloat16)
 
     ring = {}
     crossing = {}
@@ -293,16 +321,21 @@
         for copy in angles:
             copy.wait_recv()
         at, plane, column = layout(TERMS)
-        mid = slice(TERMS, 2 * TERMS)
 
         def column_of(low, own, high):
             rows = [(i, low(i + 1)) for i in range(SWEEPS)]
             rows += [(SWEEPS + x, own(x)) for x in range(WIDE)]
             return rows + [(SWEEPS + WIDE + i, high(i)) for i in range(SWEEPS)]
 
-        here = column_of(lambda x: cbox[0, x, mid], lambda x: coef[x, mid], lambda x: cbox[1, x, mid])
-        before = column_of(lambda x: dbox[0, x], lambda x: cbox[2, x, mid], lambda x: dbox[1, x])
-        after = column_of(lambda x: dbox[2, x], lambda x: cbox[3, x, mid], lambda x: dbox[3, x])
+        boxes = [mbox.at[i] for i in range(8)]
+        here, before, after = (
+            column_of(*(functools.partial(mean_plane, box) for box in group))
+            for group in (
+                (boxes[0], mrow, boxes[1]),
+                (boxes[4], boxes[2], boxes[5]),
+                (boxes[6], boxes[3], boxes[7]),
+            )
+        )
         pack = join(gather(before, plane), gather(here, plane), gather(after, plane), at, column)
         for d, other in enumerate(pack_shifts(pack)):
             kpack[d] = 0.5 * (pack + other)
@@ -312,11 +345,11 @@
             for d, other in enumerate(others):
                 kw[d, i] = 0.5 * (value + other)
 
-    FOLD = HALF // 4
-
-    def spread(half):
-        rows = pl.ds(half * HALF, HALF)
-        at, plane, _ = layout(HALF)
+    FOLD = QUARTER // 4
+
+    def spread(part_of):
+        rows = pl.ds(part_of * QUARTER, QUARTER)
+        at, plane, _ = layout(QUARTER)
         own = gather([(x, wide[SWEEPS + x, rows, :]) for x in range(WIDE)], plane)
         thin_at = at[0:FOLD]
         total = None
@@ -324,26 +357,26 @@
             piece = own[g * FOLD : (g + 1) * FOLD]
             piece = pltpu.roll(piece, 32 * g, 1) if g else piece
             total = piece if total is None else jnp.where(thin_at >= 32 * g, piece, total)
-        fold[half] = total
-        moves = [
+        fold[part_of] = total
+        moves = [(fold.at[part_of], foldbox.at[part_of, i], peer) for i, peer in enumerate(corners + (yp, ym))]
+        moves += [
             (wide.at[pl.ds(WIDE, SWEEPS), rows, :], wide.at[pl.ds(0, SWEEPS), rows, :], xp),
             (wide.at[pl.ds(SWEEPS, SWEEPS), rows, :], wide.at[pl.ds(SWEEPS + WIDE, SWEEPS), rows, :], xm),
         ]
-        for i, peer in enumerate(corners + (yp, ym)):
-            moves.append((fold.at[half], foldbox.at[half, i], peer))
         return [
-            send(src, dst, wsend.at[half, i], wrecv.at[half, i], peer) for i, (src, dst, peer) in enumerate(moves)
+            send(src, dst, wsend.at[part_of, i], wrecv.at[part_of, i], peer)
+            for i, (src, dst, peer) in enumerate(moves)
         ]
 
-    def sweeps(half, moved):
+    def sweeps(part_of, moved):
         for copy in moved:
             copy.wait_recv()
-        rows = pl.ds(half * HALF, HALF)
-        at, plane, column = layout(HALF)
+        rows = pl.ds(part_of * QUARTER, QUARTER)
+        at, plane, column = layout(QUARTER)
 
         def unfold(i, shift):
             return jnp.concatenate(
-                [pltpu.roll(foldbox[half, i], (shift - 32 * g) % LANES, 1) for g in range(4)], axis=0
+                [pltpu.roll(foldbox[part_of, i], (shift - 32 * g) % LANES, 1) for g in range(4)], axis=0
             )
 
         def beside(low, mid, high):
@@ -382,64 +415,75 @@
                     corr[later, i, rows, :] = value + step
                 else:
                     x = i - SWEEPS
-                    sol[pl.ds(half * HALF * WIDE + x, HALF, stride=WIDE), :] = vp[x, rows, :] + (value + step)
+                    sol[pl.ds(part_of * QUARTER * WIDE + x, QUARTER, stride=WIDE), :] = vp[x, rows, :] + (value + step)
             if sweep < SWEEPS - 1:
                 step = advance(SPAN, pack, pack_shifts(pack), lambda d: kpack[d, 0:1, :])
                 direction[SPAN, rows, :] = step
                 corr[later, SPAN, rows, :] = pack + step
             rho = rho_next
 
-    sums = None
+    def prepare_residual():
+        fetch[4].wait()
+        for x in range(WIDE):
+            total = REACT * vp[x]
+            for d in range(4):
+                total = total + kd[d, x, TERMS : TERMS + 1, :] * diffs[d, x]
+            base[x] = right[pl.ds(x, ROWS, stride=WIDE), :] - total
+        wide_coefficients()
+
+    sums = {}
+
+    def finish(quarter):
+        first = quarter * QUARTER
+        rows = slice(first, first + QUARTER)
+        if quarter in sums:
+            sums[quarter].wait_recv()
+            total = collect(2 + quarter) + sbox[rows]
+        else:
+            settle(0)
+            total = collect(2 + quarter)
+        for x in range(WIDE):
+            value = base[x, rows, :] - total[:, x * LANES : (x + 1) * LANES]
+            wide[SWEEPS + x, rows, :] = value
+            res[pl.ds(first * WIDE + x, QUARTER, stride=WIDE), :] = value
+        return spread(quarter)
+
+    spreads = {}
     for step in PLAN:
-        if step[0] == "m":
+        what = step[0]
+        if what == "m":
             if step[1] != 4:
                 prepare(step[1])
-            multiply(step[1])
-        elif step[0] == "z":
-            forward(1, step[1], step[2])
-            forward(-1, step[1] ^ 1, step[2])
-        elif step[0] == "y":
+            multiply(step[1], ((0,), (1,), (0, 1))[step[2]])
+        elif what == "z":
+            forward(*step[1:])
+        elif what == "y":
             o = step[1]
             crossing[o] = send(
                 part.at[o, 0, pl.ds(HALF, HALF), :], ybox.at[o], ysend.at[o], yrecv.at[o], partner
             )
-        elif step[0] == "s":
-            for unit in (0, 1):
-                ysum[unit * QUARTER : (unit + 1) * QUARTER] = collect(unit)
-            sums = send(ysum, sbox, ysend.at[RING], yrecv.at[RING], partner)
+        elif what == "s":
+            i = step[1]
+            rows = pl.ds(i * QUARTER, QUARTER)
+            ysum[rows, :] = collect(i)
+            sums[i] = send(ysum.at[rows], sbox.at[rows], ysend.at[RING + i], yrecv.at[RING + i], partner)
+        elif what == "b":
+            prepare_residual()
+        elif what == "f":
+            spreads[step[1]] = finish(step[1])
         else:
-            fetch[4].wait()
-            for x in range(WIDE):
-                total = REACT * vp[x]
-                for d in range(4):
-                    total = total + kd[d, x, TERMS : TERMS + 1, :] * diffs[d, x]
-                base[x] = right[pl.ds(x, ROWS, stride=WIDE), :] - total
-            wide_coefficients()
-
-    def finish(unit, extra):
-        first = UNITS[unit][1]
-        rows = slice(first, first + QUARTER)
-        total = collect(unit)
-        if extra is not None:
-            total = total + extra
-        for x in range(WIDE):
-            value = base[x, rows, :] - total[:, x * LANES : (x + 1) * LANES]
-            wide[SWEEPS + x, rows, :] = value
-            res[pl.ds(first * WIDE + x, QUARTER, stride=WIDE), :] = value
-
-    sums.wait_recv()
-    finish(2, sbox[0:QUARTER])
-    finish(3, sbox[QUARTER:HALF])
-    early = spread(0)
-    settle(0)
-    finish(4, None)
-    finish(5, None)
-    late = spread(1)
-    sweeps(0, early)
-    sweeps(1, late)
+            sweeps(step[1], spreads[step[1]])
 
     for copy in started:
         copy.wait_send()
+
+
+def place(sol, res, sol_out, res_out, sem):
+    copies = [pltpu.make_async_copy(sol, sol_out, sem.at[0]), pltpu.make_async_copy(res, res_out, sem.at[1])]
+    for copy in copies:
+        copy.start()
+    for copy in copies:
+        copy.wait()
 
 
 def local(start_field, right_side, mean_coef, term_coef, coupling, block_mask):
@@ -471,9 +515,11 @@
             pltpu.VMEM((WIDE, ROWS, LANES), f32),
             pltpu.VMEM((4, WIDE, ROWS, LANES), f32),
             pltpu.VMEM((WIDE, ROWS, LANES), f32),
-            pltpu.VMEM((WIDE, 2 * TERMS, LANES), f32),
-            pltpu.VMEM((4, WIDE, 2 * TERMS, LANES), f32),
-            pltpu.VMEM((4, WIDE, TERMS, LANES), f32),
+            pltpu.VMEM((WIDE, TERMS, LANES), f32),
+            pltpu.VMEM((TERMS, LANES), f32),
+            pltpu.VMEM((2, TERMS, LANES), f32),
+            pltpu.VMEM((2, WIDE, TERMS, LANES), f32),
+            pltpu.VMEM((8, TERMS, LANES), f32),
             pltpu.VMEM((4, WIDE, 2 * TERMS, LANES), f32),
             pltpu.VMEM((4, WIDE + 2 * SWEEPS, TERMS, LANES), f32),
             pltpu.VMEM((4, TERMS, LANES), f32),
@@ -481,22 +527,24 @@
             pltpu.VMEM((2, ROWS, LANES), f32),
             pltpu.VMEM((2, ROWS, LANES), f32),
             pltpu.VMEM((WIDE + 2 * SWEEPS + 1, ROWS, LANES), f32),
-            pltpu.VMEM((2, HALF // 4, LANES), f32),
-            pltpu.VMEM((2, 6, HALF // 4, LANES), f32),
+            pltpu.VMEM((4, QUARTER // 4, LANES), f32),
+            pltpu.VMEM((4, 6, QUARTER // 4, LANES), f32),
             pltpu.VMEM((2, WIDE + 2 * SWEEPS + 1, ROWS, LANES), f32),
             pltpu.VMEM((WIDE + 2 * SWEEPS + 1, ROWS, LANES), f32),
             pltpu.SemaphoreType.DMA((5,)),
             pltpu.SemaphoreType.DMA((2 * RING,)),
+            pltpu.SemaphoreType.DMA((4,)),
+            pltpu.SemaphoreType.DMA((4,)),
             pltpu.SemaphoreType.DMA((8,)),
             pltpu.SemaphoreType.DMA((8,)),
             pltpu.SemaphoreType.DMA((4,)),
             pltpu.SemaphoreType.DMA((4,)),
             pltpu.SemaphoreType.DMA((len(INBOX),)),
             pltpu.SemaphoreType.DMA((len(INBOX),)),
-            pltpu.SemaphoreType.DMA((RING + 1,)),
-            pltpu.SemaphoreType.DMA((RING + 1,)),
-            pltpu.SemaphoreType.DMA((2, 8)),
-            pltpu.SemaphoreType.DMA((2, 8)),
+            pltpu.SemaphoreType.DMA((RING + 2,)),
+            pltpu.SemaphoreType.DMA((RING + 2,)),
+            pltpu.SemaphoreType.DMA((4, 8)),
+            pltpu.SemaphoreType.DMA((4, 8)),
         ],
         compiler_params=pltpu.CompilerParams(
             collective_id=0, has_side_effects=True, vmem_limit_bytes=48000 * 1024
@@ -515,6 +563,16 @@
             )
         )
     )
+    hbm = pl.BlockSpec(memory_space=pltpu.HBM)
+    sol, res = pl.pallas_call(
+        place,
+        out_shape=(flat, flat),
+        in_specs=[vmem, vmem],
+        out_specs=(hbm, hbm),
+        scratch_shapes=[pltpu.SemaphoreType.DMA((2,))],
+        compiler_params=pltpu.CompilerParams(vmem_limit_bytes=1 << 20),
+        name="place",
+    )(sol, res)
     return (sol.reshape(start_field.shape), res.reshape(start_field.shape))
 
 

time: 59.8 us -> 56.1 us (0.938)
  Pallas kernels: 57.6 us -> 55.3 us
  local copies, waits for them, and re-layouts: 1.41 us -> 0 us
    pallas_call x1, Pallas kernels: 57.6 us -> 54.5 us  [local(): pl.pallas_call(kernel, out_shape=(flat, flat), in_specs=[pl.BlockSpec(mem...]
    unnamed x2 -> x0, local copies, waits for them, and re-layouts: 1.41 us -> none
    pallas_call x0 -> x1, Pallas kernels: none -> 0.81 us  [local(): pl.pallas_call(place, out_shape=(flat, flat), in_specs=[vmem, vmem], out_...]
where the time goes in v5:
time: 56.1 us; the launch traced here: 56 us
  Pallas kernels  55.3 us (99%)
  between operations  0.64 us (1%)
    pallas_call x1, Pallas kernels, local(): pl.pallas_call(kernel, out_shape=(flat, flat), in_specs=[pl.BlockSpec(mem...  54.5 us

profile of v5, /device:TPU:1, one launch (start us, length us, event | category | flops | bytes accessed | tf_op | source)
XLA Modules:
  0.0 56.0 jit_solution(524230852427207162)
XLA Ops:
  0.6 54.5 %galerkin_step.1 = (f32[512,128]{1,0:T(8,128)S(1)}, f32[512,128]{1,0:T(8,128)S(1)}) custom-call(f32[512,128]{1,0:T(8,128)} %bitcast.5, f32[512,128]{1,0:T(8,128)} %bitcast.6, f32[4,128]{1,0:T(4,128)} %mean_in.1, f32[32,128]{1,0:T(8,128)} %bitcast.7, f32[8,2048,128]{2,1,0:T(8,128)} %coupling.1, s32[8,16,16]{2,1,0:T(8,128)} %mask_in.1), custom_call_target="tpu_custom_call" | custom-call | tf_op jit(solution)/shard_map/galerkin_step/pallas_call | solution.py:494
  55.2 0.8 %place.1 = (f32[512,128]{1,0:T(8,128)}, f32[512,128]{1,0:T(8,128)}) custom-call(f32[512,128]{1,0:T(8,128)S(1)} %get-tuple-element.6.sol, f32[512,128]{1,0:T(8,128)S(1)} %get-tuple-element.7.res), custom_call_target="tpu_custom_call" | custom-call | tf_op jit(solution)/shard_map/place/pallas_call | solution.py:567

commit v6 on v5

--- a/solution.py
+++ b/solution.py
@@ -15,26 +15,36 @@
 RING = 8
 GROUPS = 2
 ROWS = 128
-HALF = 64
 WIDE = 4
 LANES = 128
 CELLS = WIDE * LANES
 TERMS = 8
 
-QUARTER = 32
-UNITS = tuple((p, r, QUARTER, way) for p, r in ((0, 0), (1, 0), (1, HALF)) for r, way in ((r, 1), (r + QUARTER, -1)))
+EARLY = (32, 24)
+LATE = (32, 40)
+CROSSING = sum(EARLY)
+UNITS = tuple(
+    (p, first + (rows[0] if way < 0 else 0), rows[way < 0], way)
+    for p, first, rows in ((0, 0, EARLY), (1, 0, EARLY), (1, CROSSING, LATE))
+    for way in (1, -1)
+)
+MOST = max(EARLY + LATE)
+GROUP = WIDE * 2 * SWEEPS
 
 PLAN = (
-    ("m", 4, 0), ("y", 4), ("z", 1, 0, 4), ("z", -1, 1, 4), ("m", 4, 1), ("z", 1, 2, 4), ("z", -1, 3, 4),
-    ("m", 3, 2), ("y", 3), ("z", 1, 3, 3), ("m", 5, 2), ("y", 5), ("z", -1, 0, 3), ("z", 1, 1, 3), ("z", -1, 2, 3),
-    ("m", 2, 2), ("y", 2), ("m", 6, 2), ("y", 6), ("z", 1, 0, 3), ("z", -1, 1, 3), ("m", 1, 2), ("y", 1),
-    ("z", 1, 4, 4), ("z", -1, 5, 4), ("m", 7, 2), ("y", 7), ("z", 1, 2, 3), ("z", -1, 3, 3), ("m", 0, 2),
-    ("z", -1, 0, 2), ("z", 1, 3, 2), ("b",), ("z", 1, 1, 2), ("z", -1, 2, 2), ("z", 1, 0, 2), ("z", -1, 1, 2),
-    ("z", 1, 4, 3), ("z", -1, 4, 3), ("z", 1, 5, 3), ("z", -1, 5, 3), ("z", 1, 2, 2), ("z", -1, 0, 1),
-    ("z", 1, 1, 1), ("z", -1, 3, 2), ("z", 1, 0, 1), ("z", -1, 1, 1), ("y", 0), ("z", 1, 4, 2), ("z", -1, 4, 2),
-    ("z", 1, 5, 2), ("z", -1, 5, 2), ("z", 1, 2, 1), ("z", -1, 2, 1), ("z", 1, 3, 1), ("z", -1, 3, 1), ("s", 0),
-    ("s", 1), ("z", 1, 4, 1), ("z", -1, 4, 1), ("z", 1, 5, 1), ("z", -1, 5, 1), ("f", 0), ("f", 1), ("f", 2),
-    ("f", 3), ("c", 0), ("c", 1), ("c", 2), ("c", 3),
+    ("m", 4, 0, 0), ("z", 1, 0, 4, 0), ("z", -1, 1, 4, 0), ("y", 4, 0), ("m", 4, 1, 0), ("z", 1, 2, 4, 0),
+    ("z", -1, 3, 4, 0), ("x",), ("m", 4, 2, 1), ("z", 1, 0, 4, 1), ("z", -1, 1, 4, 1), ("z", 1, 2, 4, 1),
+    ("z", -1, 3, 4, 1), ("y", 4, 1), ("m", 3, 2, 2), ("y", 3, 2), ("z", 1, 1, 3, 2), ("z", 1, 3, 3, 2),
+    ("m", 5, 2, 2), ("y", 5, 2), ("z", -1, 0, 3, 2), ("z", -1, 2, 3, 2), ("m", 2, 2, 2), ("y", 2, 2),
+    ("m", 6, 2, 2), ("y", 6, 2), ("z", -1, 1, 3, 2), ("z", 1, 0, 3, 2), ("m", 1, 2, 2), ("y", 1, 2),
+    ("z", -1, 5, 4, 2), ("z", 1, 4, 4, 2), ("m", 7, 2, 2), ("y", 7, 2), ("z", -1, 3, 3, 2), ("z", 1, 3, 2, 2),
+    ("m", 0, 2, 2), ("z", 1, 1, 2, 2), ("z", -1, 0, 2, 2), ("z", 1, 2, 3, 2), ("b",), ("z", -1, 2, 2, 2),
+    ("z", 1, 0, 2, 2), ("z", -1, 1, 2, 2), ("z", 1, 5, 3, 2), ("z", -1, 5, 3, 2), ("z", 1, 4, 3, 2),
+    ("z", -1, 4, 3, 2), ("z", 1, 1, 1, 2), ("z", -1, 0, 1, 2), ("z", 1, 2, 2, 2), ("z", -1, 3, 2, 2), ("y", 0, 2),
+    ("z", 1, 0, 1, 2), ("z", -1, 1, 1, 2), ("z", 1, 5, 2, 2), ("z", -1, 5, 2, 2), ("z", 1, 4, 2, 2),
+    ("z", -1, 4, 2, 2), ("z", 1, 3, 1, 2), ("z", -1, 2, 1, 2), ("z", 1, 2, 1, 2), ("z", -1, 3, 1, 2), ("s", 0),
+    ("s", 1), ("z", 1, 5, 1, 2), ("z", -1, 5, 1, 2), ("z", 1, 4, 1, 2), ("z", -1, 4, 1, 2), ("f", 0), ("f", 1),
+    ("f", 3), ("f", 2), ("c", 0), ("c", 1), ("c", 3), ("c", 2),
 )
 
 
@@ -43,9 +53,27 @@
 
 
 INBOX = {}
+PLACE = {}
 for step_ in PLAN:
     if step_[0] == "z":
-        INBOX[(step_[1], step_[2], step_[3] - 1)] = len(INBOX)
+        INBOX.setdefault((step_[1], step_[2], step_[3] - 1), len(INBOX))
+        PLACE[step_[1:]] = len(PLACE)
+CROSS = {step_[1:]: i for i, step_ in enumerate(step_ for step_ in PLAN if step_[0] == "y")}
+ORDER = (1, 2, 0, 3)
+
+
+def columns(x):
+    at = ORDER.index(x) * LANES
+    return slice(at, at + LANES)
+
+
+def cells(group):
+    return (slice(0, 2 * LANES), slice(2 * LANES, CELLS), slice(0, CELLS))[group]
+
+
+def span(group):
+    cols = cells(group)
+    return pl.ds(cols.start, cols.stop - cols.start)
 
 
 def kernel(
@@ -109,8 +137,17 @@
             hi_x = pltpu.roll(planes[x], x + 1, 1)
             low = lo_x if x == 0 else jnp.where(lane == x, lo_x, low)
             high = hi_x if x == 0 else jnp.where(lane == x, hi_x, high)
-        edge[0] = low
-        edge[1] = high
+        for i, value in enumerate((low, high)):
+            total = value[0:8]
+            for g in range(1, ROWS // 8):
+                piece = pltpu.roll(value[g * 8 : (g + 1) * 8], 8 * g, 1)
+                total = jnp.where(lane[0:8] >= 8 * g, piece, total)
+            edge[i] = total
+
+    def unfolded(box, to, x):
+        return jnp.concatenate(
+            [pltpu.roll(box, (to - x - 8 * g) % LANES, 1) for g in range(ROWS // 8)], axis=0
+        )
 
     started = []
 
@@ -126,8 +163,8 @@
         center = vp[x]
         up = vp[x - 1] if x > 0 else rowbox[0]
         down = vp[x + 1] if x < WIDE - 1 else rowbox[1]
-        lo_col = colbox[0] if x == 0 else pltpu.roll(colbox[0], LANES - x, 1)
-        hi_col = pltpu.roll(colbox[1], LANES - 1 - x, 1)
+        lo_col = unfolded(colbox[0], 0, x)
+        hi_col = unfolded(colbox[1], LANES - 1, x)
         left = jnp.where(lane == 0, lo_col, pltpu.roll(center, 1, 1))
         after = jnp.where(lane == LANES - 1, hi_col, pltpu.roll(center, LANES - 1, 1))
         return (center - up, center - down, center - left, center - after)
@@ -138,30 +175,32 @@
         plane = field[pl.ds(x, ROWS, stride=WIDE), :]
         vp[x] = plane
         values.append(plane)
+
+    pl.semaphore_wait(barrier, len(peers))
+
+    halo = [
+        send(vp.at[WIDE - 1], rowbox.at[0], hsend.at[0], hrecv.at[0], xp),
+        send(vp.at[0], rowbox.at[1], hsend.at[1], hrecv.at[1], xm),
+    ]
     edges(values)
+    halo += [
+        send(edge.at[1], colbox.at[0], hsend.at[2], hrecv.at[2], yp),
+        send(edge.at[0], colbox.at[1], hsend.at[3], hrecv.at[3], ym),
+    ]
     fetch[1].wait()
     fetch[2].wait()
     for x in range(WIDE):
         coef[x] = terms[pl.ds(x, TERMS, stride=WIDE), :]
     mrow[0:WIDE] = mean[...]
     mrow[WIDE:] = mean[...]
-
-    pl.semaphore_wait(barrier, len(peers))
-
     coefs = [
+        send(coef, cybox.at[0], csend.at[2], crecv.at[2], yp),
+        send(coef, cybox.at[1], csend.at[3], crecv.at[3], ym),
         send(coef.at[WIDE - 1], cxbox.at[0], csend.at[0], crecv.at[0], xp),
         send(coef.at[0], cxbox.at[1], csend.at[1], crecv.at[1], xm),
-        send(coef, cybox.at[0], csend.at[2], crecv.at[2], yp),
-        send(coef, cybox.at[1], csend.at[3], crecv.at[3], ym),
     ]
     means = [
         send(mrow, mbox.at[i], msend.at[i], mrecv.at[i], peer) for i, peer in enumerate((xp, xm, yp, ym))
-    ]
-    halo = [
-        send(vp.at[WIDE - 1], rowbox.at[0], hsend.at[0], hrecv.at[0], xp),
-        send(vp.at[0], rowbox.at[1], hsend.at[1], hrecv.at[1], xm),
-        send(edge.at[1], colbox.at[0], hsend.at[2], hrecv.at[2], yp),
-        send(edge.at[0], colbox.at[1], hsend.at[3], hrecv.at[3], ym),
     ]
     angles = [
         send(mrow, mbox.at[4 + i], msend.at[4 + i], mrecv.at[4 + i], corner) for i, corner in enumerate(corners)
@@ -178,10 +217,10 @@
                 lhs_hi[o, p * ROWS : (p + 1) * ROWS, t * ROWS : (t + 1) * ROWS] = high
                 lhs_lo[o, p * ROWS : (p + 1) * ROWS, t * ROWS : (t + 1) * ROWS] = low
 
-    def multiply(o, parts):
+    def multiply(o, parts, groups):
         first, last = parts[0] * ROWS, (parts[-1] + 1) * ROWS
-        for n in range(2):
-            cols = slice(n * 2 * LANES, (n + 1) * 2 * LANES)
+        for group in groups:
+            cols = cells(group)
             dot = functools.partial(jnp.dot, preferred_element_type=jnp.float32)
             total = (
                 dot(lhs_hi[o, first:last], f_hi[:, cols])
@@ -194,46 +233,47 @@
     fetch[3].wait()
     prepare(4)
 
-    for copy in coefs + means:
-        copy.wait_recv()
-
     def mean_plane(box, x):
         return jnp.broadcast_to(box[x : x + 1, :], (TERMS, LANES))
 
     thin = lax.broadcasted_iota(jnp.int32, (TERMS, LANES), 1)
 
     def coefficients(x, rows, own, low, high, before, after):
-        up = own(x - 1) if x > 0 else low
-        down = own(x + 1) if x < WIDE - 1 else high
+        up = own(x - 1) if x > 0 else low()
+        down = own(x + 1) if x < WIDE - 1 else high()
         here = own(x)
         left = jnp.where(thin == 0, pltpu.roll(before(x), 1, 1), pltpu.roll(here, 1, 1))
         right_of = jnp.where(thin == LANES - 1, pltpu.roll(after(x), LANES - 1, 1), pltpu.roll(here, LANES - 1, 1))
         for d, other in enumerate((up, down, left, right_of)):
             kd[d, x, rows, :] = 0.5 * (here + other)
 
-    for x in range(WIDE):
-        coefficients(
-            x, slice(0, TERMS), lambda i: coef[i], cxbox[0], cxbox[1], lambda i: cybox[0, i], lambda i: cybox[1, i]
-        )
-        coefficients(
-            x,
-            slice(TERMS, 2 * TERMS),
-            lambda i: mean_plane(mrow, i),
-            mean_plane(mbox.at[0], WIDE - 1),
-            mean_plane(mbox.at[1], 0),
-            lambda i: mean_plane(mbox.at[2], i),
-            lambda i: mean_plane(mbox.at[3], i),
-        )
-
-    for copies, planes in ((halo[2:], (1, 2)), (halo[:2], (0, 3))):
+    def fluxes(copies, planes):
         for copy in copies:
             copy.wait_recv()
         for x in planes:
+            coefficients(
+                x,
+                slice(0, TERMS),
+                lambda i: coef[i],
+                lambda: cxbox[0],
+                lambda: cxbox[1],
+                lambda i: cybox[0, i],
+                lambda i: cybox[1, i],
+            )
+            coefficients(
+                x,
+                slice(TERMS, 2 * TERMS),
+                lambda i: mean_plane(mrow, i),
+                lambda: mean_plane(mbox.at[0], WIDE - 1),
+                lambda: mean_plane(mbox.at[1], 0),
+                lambda i: mean_plane(mbox.at[2], i),
+                lambda i: mean_plane(mbox.at[3], i),
+            )
             for d, delta in enumerate(differences(x)):
                 diffs[d, x] = delta
 
         @pl.loop(0, TERMS)
-        def _(t, planes=planes):
+        def _(t):
             rows = pl.ds(pl.multiple_of(t * ROWS, ROWS), ROWS)
             for x in planes:
                 total = None
@@ -241,9 +281,10 @@
                     piece = kd[d, x, pl.ds(t, 1), :] * diffs[d, x]
                     total = piece if total is None else total + piece
                 high = total.astype(jnp.bfloat16)
-                cols = slice(x * LANES, (x + 1) * LANES)
-                f_hi[rows, cols] = high
-                f_lo[rows, cols] = (total - high.astype(jnp.float32)).astype(jnp.bfloat16)
+                f_hi[rows, columns(x)] = high
+                f_lo[rows, columns(x)] = (total - high.astype(jnp.float32)).astype(jnp.bfloat16)
+
+    fluxes(halo[2:] + coefs[:2] + means[2:], (1, 2))
 
     ring = {}
     crossing = {}
@@ -252,34 +293,41 @@
     def settle(o):
         if o not in crossed:
             crossed.add(o)
-            crossing[o].wait_recv()
-            part[o, 1, HALF:, :] += ybox[o]
-
-    def forward(way, unit, o):
+            for copy in crossing[o]:
+                copy.wait_recv()
+            part[o, 1, CROSSING:, :] += ybox[o]
+
+    def arrived(way, unit, o):
+        for copy in ring[(way, unit, o)]:
+            copy.wait_recv()
+
+    def forward(way, unit, o, group):
         p, first, count, _ = UNITS[unit]
         at = (o * way) % RING
         if unit >= 4:
             settle(at)
         if o < hops(unit, way):
-            ring[(way, unit, o)].wait_recv()
-            part[at, p, first : first + count, :] += inbox[INBOX[(way, unit, o)]]
-        i = INBOX[(way, unit, o - 1)]
-        ring[(way, unit, o - 1)] = send(
-            part.at[at, p, pl.ds(first, count), :],
-            inbox.at[i],
+            arrived(way, unit, o)
+            part[at, p, first : first + count, :] += inbox[INBOX[(way, unit, o)], 0:count]
+        i = PLACE[(way, unit, o, group)]
+        cols = span(group)
+        copy = send(
+            part.at[at, p, pl.ds(first, count), cols],
+            inbox.at[INBOX[(way, unit, o - 1)], pl.ds(0, count), cols],
             rsend.at[i],
             rrecv.at[i],
             zp if way == 1 else zm,
         )
+        ring.setdefault((way, unit, o - 1), []).append(copy)
 
     def collect(unit):
         p, first, count, _ = UNITS[unit]
         for way in (1, -1):
-            ring[(way, unit, 0)].wait_recv()
+            arrived(way, unit, 0)
         return (
             part[0, p, first : first + count, :]
-            + inbox[INBOX[(1, unit, 0)]]
-            + inbox[INBOX[(-1, unit, 0)]]
+            + inbox[INBOX[(1, unit, 0)], 0:count]
+            + inbox[INBOX[(-1, unit, 0)], 0:count]
         )
 
     SPAN = WIDE + 2 * SWEEPS
@@ -345,18 +393,16 @@
             for d, other in enumerate(others):
                 kw[d, i] = 0.5 * (value + other)
 
-    FOLD = QUARTER // 4
-
     def spread(part_of):
-        rows = pl.ds(part_of * QUARTER, QUARTER)
-        at, plane, _ = layout(QUARTER)
+        _, first, count, _ = UNITS[2 + part_of]
+        rows = pl.ds(first, count)
+        at, plane, _ = layout(count)
         own = gather([(x, wide[SWEEPS + x, rows, :]) for x in range(WIDE)], plane)
-        thin_at = at[0:FOLD]
-        total = None
-        for g in range(4):
-            piece = own[g * FOLD : (g + 1) * FOLD]
-            piece = pltpu.roll(piece, 32 * g, 1) if g else piece
-            total = piece if total is None else jnp.where(thin_at >= 32 * g, piece, total)
+        thin_at = at[0:8]
+        total = own[0:8]
+        for g in range(1, count // 8):
+            piece = pltpu.roll(own[g * 8 : (g + 1) * 8], GROUP * g, 1)
+            total = jnp.where(thin_at >= GROUP * g, piece, total)
         fold[part_of] = total
         moves = [(fold.at[part_of], foldbox.at[part_of, i], peer) for i, peer in enumerate(corners + (yp, ym))]
         moves += [
@@ -371,12 +417,13 @@
     def sweeps(part_of, moved):
         for copy in moved:
             copy.wait_recv()
-        rows = pl.ds(part_of * QUARTER, QUARTER)
-        at, plane, column = layout(QUARTER)
+        _, first, count, _ = UNITS[2 + part_of]
+        rows = pl.ds(first, count)
+        at, plane, column = layout(count)
 
         def unfold(i, shift):
             return jnp.concatenate(
-                [pltpu.roll(foldbox[part_of, i], (shift - 32 * g) % LANES, 1) for g in range(4)], axis=0
+                [pltpu.roll(foldbox[part_of, i], (shift - GROUP * g) % LANES, 1) for g in range(count // 8)], axis=0
             )
 
         def beside(low, mid, high):
@@ -415,7 +462,7 @@
                     corr[later, i, rows, :] = value + step
                 else:
                     x = i - SWEEPS
-                    sol[pl.ds(part_of * QUARTER * WIDE + x, QUARTER, stride=WIDE), :] = vp[x, rows, :] + (value + step)
+                    sol[pl.ds(first * WIDE + x, count, stride=WIDE), :] = vp[x, rows, :] + (value + step)
             if sweep < SWEEPS - 1:
                 step = advance(SPAN, pack, pack_shifts(pack), lambda d: kpack[d, 0:1, :])
                 direction[SPAN, rows, :] = step
@@ -434,8 +481,8 @@
     sums = {}
 
     def finish(quarter):
-        first = quarter * QUARTER
-        rows = slice(first, first + QUARTER)
+        _, first, count, _ = UNITS[2 + quarter]
+        rows = slice(first, first + count)
         if quarter in sums:
             sums[quarter].wait_recv()
             total = collect(2 + quarter) + sbox[rows]
@@ -443,9 +490,9 @@
             settle(0)
             total = collect(2 + quarter)
         for x in range(WIDE):
-            value = base[x, rows, :] - total[:, x * LANES : (x + 1) * LANES]
+            value = base[x, rows, :] - total[:, columns(x)]
             wide[SWEEPS + x, rows, :] = value
-            res[pl.ds(first * WIDE + x, QUARTER, stride=WIDE), :] = value
+            res[pl.ds(first * WIDE + x, count, stride=WIDE), :] = value
         return spread(quarter)
 
     spreads = {}
@@ -454,19 +501,22 @@
         if what == "m":
             if step[1] != 4:
                 prepare(step[1])
-            multiply(step[1], ((0,), (1,), (0, 1))[step[2]])
+            multiply(step[1], ((0,), (1,), (0, 1))[step[2]], ((0,), (1,), (0, 1))[step[3]])
         elif what == "z":
             forward(*step[1:])
         elif what == "y":
-            o = step[1]
-            crossing[o] = send(
-                part.at[o, 0, pl.ds(HALF, HALF), :], ybox.at[o], ysend.at[o], yrecv.at[o], partner
+            o, cols, i = step[1], span(step[2]), CROSS[step[1:]]
+            copy = send(
+                part.at[o, 0, pl.ds(CROSSING, ROWS - CROSSING), cols], ybox.at[o, :, cols], ysend.at[i], yrecv.at[i], partner
             )
+            crossing.setdefault(o, []).append(copy)
         elif what == "s":
             i = step[1]
-            rows = pl.ds(i * QUARTER, QUARTER)
+            rows = pl.ds(UNITS[i][1], UNITS[i][2])
             ysum[rows, :] = collect(i)
-            sums[i] = send(ysum.at[rows], sbox.at[rows], ysend.at[RING + i], yrecv.at[RING + i], partner)
+            sums[i] = send(ysum.at[rows], sbox.at[rows], ysend.at[len(CROSS) + i], yrecv.at[len(CROSS) + i], partner)
+        elif what == "x":
+            fluxes(halo[:2] + coefs[2:] + means[:2], (0, 3))
         elif what == "b":
             prepare_residual()
         elif what == "f":
@@ -508,10 +558,10 @@
             pltpu.VMEM((TERMS * ROWS, CELLS), bf16),
             pltpu.VMEM((TERMS * ROWS, CELLS), bf16),
             pltpu.VMEM((RING, 2, ROWS, CELLS), f32),
-            pltpu.VMEM((len(INBOX), QUARTER, CELLS), f32),
-            pltpu.VMEM((HALF, CELLS), f32),
-            pltpu.VMEM((RING, HALF, CELLS), f32),
-            pltpu.VMEM((HALF, CELLS), f32),
+            pltpu.VMEM((len(INBOX), MOST, CELLS), f32),
+            pltpu.VMEM((CROSSING, CELLS), f32),
+            pltpu.VMEM((RING, ROWS - CROSSING, CELLS), f32),
+            pltpu.VMEM((CROSSING, CELLS), f32),
             pltpu.VMEM((WIDE, ROWS, LANES), f32),
             pltpu.VMEM((4, WIDE, ROWS, LANES), f32),
             pltpu.VMEM((WIDE, ROWS, LANES), f32),
@@ -523,12 +573,12 @@
             pltpu.VMEM((4, WIDE, 2 * TERMS, LANES), f32),
             pltpu.VMEM((4, WIDE + 2 * SWEEPS, TERMS, LANES), f32),
             pltpu.VMEM((4, TERMS, LANES), f32),
+            pltpu.VMEM((2, 8, LANES), f32),
             pltpu.VMEM((2, ROWS, LANES), f32),
-            pltpu.VMEM((2, ROWS, LANES), f32),
-            pltpu.VMEM((2, ROWS, LANES), f32),
+            pltpu.VMEM((2, 8, LANES), f32),
             pltpu.VMEM((WIDE + 2 * SWEEPS + 1, ROWS, LANES), f32),
-            pltpu.VMEM((4, QUARTER // 4, LANES), f32),
-            pltpu.VMEM((4, 6, QUARTER // 4, LANES), f32),
+            pltpu.VMEM((4, 8, LANES), f32),
+            pltpu.VMEM((4, 6, 8, LANES), f32),
             pltpu.VMEM((2, WIDE + 2 * SWEEPS + 1, ROWS, LANES), f32),
             pltpu.VMEM((WIDE + 2 * SWEEPS + 1, ROWS, LANES), f32),
             pltpu.SemaphoreType.DMA((5,)),
@@ -539,10 +589,10 @@
             pltpu.SemaphoreType.DMA((8,)),
             pltpu.SemaphoreType.DMA((4,)),
             pltpu.SemaphoreType.DMA((4,)),
-            pltpu.SemaphoreType.DMA((len(INBOX),)),
-            pltpu.SemaphoreType.DMA((len(INBOX),)),
-            pltpu.SemaphoreType.DMA((RING + 2,)),
-            pltpu.SemaphoreType.DMA((RING + 2,)),
+            pltpu.SemaphoreType.DMA((len(PLACE),)),
+            pltpu.SemaphoreType.DMA((len(PLACE),)),
+            pltpu.SemaphoreType.DMA((len(CROSS) + 2,)),
+            pltpu.SemaphoreType.DMA((len(CROSS) + 2,)),
             pltpu.SemaphoreType.DMA((4, 8)),
             pltpu.SemaphoreType.DMA((4, 8)),
         ],

time: 56.1 us -> 55.5 us (0.989)
  no operation moved by 1% of the time
where the time goes in v6:
time: 55.5 us; the launch traced here: 55.4 us
  Pallas kernels  54.8 us (99%)
  between operations  0.64 us (1%)
    pallas_call x1, Pallas kernels, local(): pl.pallas_call(kernel, out_shape=(flat, flat), in_specs=[pl.BlockSpec(mem...  54 us

profile of v6, /device:TPU:1, one launch (start us, length us, event | category | flops | bytes accessed | tf_op | source)
XLA Modules:
  0.0 55.4 jit_solution(15430257070950576148)
XLA Ops:
  0.6 54.0 %galerkin_step.1 = (f32[512,128]{1,0:T(8,128)S(1)}, f32[512,128]{1,0:T(8,128)S(1)}) custom-call(f32[512,128]{1,0:T(8,128)} %bitcast.5, f32[512,128]{1,0:T(8,128)} %bitcast.6, f32[4,128]{1,0:T(4,128)} %mean_in.1, f32[32,128]{1,0:T(8,128)} %bitcast.7, f32[8,2048,128]{2,1,0:T(8,128)} %coupling.1, s32[8,16,16]{2,1,0:T(8,128)} %mask_in.1), custom_call_target="tpu_custom_call" | custom-call | tf_op jit(solution)/shard_map/galerkin_step/pallas_call | solution.py:544
  54.6 0.8 %place.1 = (f32[512,128]{1,0:T(8,128)}, f32[512,128]{1,0:T(8,128)}) custom-call(f32[512,128]{1,0:T(8,128)S(1)} %get-tuple-element.6.sol, f32[512,128]{1,0:T(8,128)S(1)} %get-tuple-element.7.res), custom_call_target="tpu_custom_call" | custom-call | tf_op jit(solution)/shard_map/place/pallas_call | solution.py:617

commit v7 on v6

--- a/solution.py
+++ b/solution.py
@@ -36,14 +36,14 @@
     ("z", -1, 3, 4, 0), ("x",), ("m", 4, 2, 1), ("z", 1, 0, 4, 1), ("z", -1, 1, 4, 1), ("z", 1, 2, 4, 1),
     ("z", -1, 3, 4, 1), ("y", 4, 1), ("m", 3, 2, 2), ("y", 3, 2), ("z", 1, 1, 3, 2), ("z", 1, 3, 3, 2),
     ("m", 5, 2, 2), ("y", 5, 2), ("z", -1, 0, 3, 2), ("z", -1, 2, 3, 2), ("m", 2, 2, 2), ("y", 2, 2),
-    ("m", 6, 2, 2), ("y", 6, 2), ("z", -1, 1, 3, 2), ("z", 1, 0, 3, 2), ("m", 1, 2, 2), ("y", 1, 2),
-    ("z", -1, 5, 4, 2), ("z", 1, 4, 4, 2), ("m", 7, 2, 2), ("y", 7, 2), ("z", -1, 3, 3, 2), ("z", 1, 3, 2, 2),
-    ("m", 0, 2, 2), ("z", 1, 1, 2, 2), ("z", -1, 0, 2, 2), ("z", 1, 2, 3, 2), ("b",), ("z", -1, 2, 2, 2),
-    ("z", 1, 0, 2, 2), ("z", -1, 1, 2, 2), ("z", 1, 5, 3, 2), ("z", -1, 5, 3, 2), ("z", 1, 4, 3, 2),
-    ("z", -1, 4, 3, 2), ("z", 1, 1, 1, 2), ("z", -1, 0, 1, 2), ("z", 1, 2, 2, 2), ("z", -1, 3, 2, 2), ("y", 0, 2),
-    ("z", 1, 0, 1, 2), ("z", -1, 1, 1, 2), ("z", 1, 5, 2, 2), ("z", -1, 5, 2, 2), ("z", 1, 4, 2, 2),
-    ("z", -1, 4, 2, 2), ("z", 1, 3, 1, 2), ("z", -1, 2, 1, 2), ("z", 1, 2, 1, 2), ("z", -1, 3, 1, 2), ("s", 0),
-    ("s", 1), ("z", 1, 5, 1, 2), ("z", -1, 5, 1, 2), ("z", 1, 4, 1, 2), ("z", -1, 4, 1, 2), ("f", 0), ("f", 1),
+    ("m", 6, 2, 2), ("y", 6, 2), ("z", 1, 0, 3, 2), ("z", -1, 1, 3, 2), ("m", 1, 2, 2), ("y", 1, 2),
+    ("z", -1, 5, 4, 2), ("z", 1, 4, 4, 2), ("m", 7, 2, 2), ("y", 7, 2), ("z", 1, 1, 2, 2), ("z", -1, 3, 3, 2),
+    ("z", 1, 3, 2, 2), ("m", 0, 2, 2), ("z", 1, 2, 3, 2), ("z", -1, 0, 2, 2), ("b",), ("z", -1, 2, 2, 2),
+    ("z", 1, 0, 2, 2), ("z", -1, 1, 2, 2), ("z", 1, 5, 3, 2), ("z", -1, 5, 3, 2), ("z", 1, 1, 1, 2),
+    ("z", -1, 4, 3, 2), ("z", 1, 4, 3, 2), ("z", -1, 0, 1, 2), ("z", 1, 2, 2, 2), ("z", -1, 3, 2, 2),
+    ("z", 1, 0, 1, 2), ("z", -1, 1, 1, 2), ("z", 1, 5, 2, 2), ("y", 0, 2), ("z", -1, 5, 2, 2), ("z", 1, 3, 1, 2),
+    ("z", -1, 4, 2, 2), ("z", 1, 4, 2, 2), ("z", -1, 2, 1, 2), ("z", 1, 2, 1, 2), ("s", 0), ("z", -1, 3, 1, 2),
+    ("s", 1), ("z", 1, 5, 1, 2), ("z", -1, 5, 1, 2), ("z", -1, 4, 1, 2), ("z", 1, 4, 1, 2), ("f", 0), ("f", 1),
     ("f", 3), ("f", 2), ("c", 0), ("c", 1), ("c", 3), ("c", 2),
 )
 

time: 55.5 us -> 55.5 us (level)
  no operation moved by 1% of the time
where the time goes in v7:
time: 55.5 us; the launch traced here: 55.4 us
  Pallas kernels  54.8 us (99%)
  between operations  0.64 us (1%)
    pallas_call x1, Pallas kernels, local(): pl.pallas_call(kernel, out_shape=(flat, flat), in_specs=[pl.BlockSpec(mem...  54 us

profile of v7, /device:TPU:1, one launch (start us, length us, event | category | flops | bytes accessed | tf_op | source)
XLA Modules:
  0.0 55.4 jit_solution(13745494393337637291)
XLA Ops:
  0.6 54.0 %galerkin_step.1 = (f32[512,128]{1,0:T(8,128)S(1)}, f32[512,128]{1,0:T(8,128)S(1)}) custom-call(f32[512,128]{1,0:T(8,128)} %bitcast.5, f32[512,128]{1,0:T(8,128)} %bitcast.6, f32[4,128]{1,0:T(4,128)} %mean_in.1, f32[32,128]{1,0:T(8,128)} %bitcast.7, f32[8,2048,128]{2,1,0:T(8,128)} %coupling.1, s32[8,16,16]{2,1,0:T(8,128)} %mask_in.1), custom_call_target="tpu_custom_call" | custom-call | tf_op jit(solution)/shard_map/galerkin_step/pallas_call | solution.py:544
  54.6 0.8 %place.1 = (f32[512,128]{1,0:T(8,128)}, f32[512,128]{1,0:T(8,128)}) custom-call(f32[512,128]{1,0:T(8,128)S(1)} %get-tuple-element.6.sol, f32[512,128]{1,0:T(8,128)S(1)} %get-tuple-element.7.res), custom_call_target="tpu_custom_call" | custom-call | tf_op jit(solution)/shard_map/place/pallas_call | solution.py:617
